TPU v7x, 256 devices: a whole 4x4x8 slice. The times are simulated.
256 devices in a mesh: row: 8 (over y, core), col: 32 (over x, z).
Axes of the slice: x: 4, y: 4, z: 8, core: 2. Of those that a mesh axis runs over, the one named last changes fastest.
Arguments:
- images: float32 [4, 256, 65536], P(None, 'row', 'col'), may hold values from -6 to 6
Outputs:
- coefficients: float32 [4, 256, 65536], P(None, 'row', 'col')
All inputs are finite; a program needn't handle non-finite values.
Results may differ from a plain program's by a relative error of at most 0.00002.
Values sent between devices are 32-bit elements; how exact they have to be, the bound alone decides.
No kernel may reach another device: no remote copies, remote signals or barrier semaphores. Data moves between devices by JAX's collectives and lax.ppermute only.
A program may use at most 128 MiB of HBM per device.

v0:
```python
import jax
import jax.numpy as jnp
from jax import lax
from jax.sharding import PartitionSpec as P

LEVELS = 3


PREDICT_ONE = -1.586134342
UPDATE_ONE = -0.05298011854
PREDICT_TWO = 0.8829110762
UPDATE_TWO = 0.4435068522
SCALE_HIGH = 1.230174105
SCALE_LOW = 1.0 / 1.230174105


def with_halo(block, sides, width):
    for axis, dim in sides:
        count = lax.axis_size(axis)
        forward = [(i, i + 1) for i in range(count - 1)]
        backward = [(target, source) for source, target in forward]
        low = lax.ppermute(
            lax.slice_in_dim(block, block.shape[dim] - width, None, axis=dim), axis, forward
        )
        high = lax.ppermute(lax.slice_in_dim(block, 0, width, axis=dim), axis, backward)
        block = jnp.concatenate([low, block, high], axis=dim)
    return block


def segment(values, start, stop, along):
    return lax.slice_in_dim(values, start, stop, 1, along)


def lifting(extended, along):
    length = extended.shape[along]
    halves = length // 2
    evens = lax.slice_in_dim(extended, 0, length, 2, along)
    odds = lax.slice_in_dim(extended, 1, length, 2, along)
    predicted = segment(odds, 0, halves - 1, along) + PREDICT_ONE * (
        segment(evens, 0, halves - 1, along) + segment(evens, 1, halves, along)
    )
    updated = segment(evens, 1, halves - 1, along) + UPDATE_ONE * (
        segment(predicted, 0, halves - 2, along) + segment(predicted, 1, halves - 1, along)
    )
    refined = segment(predicted, 1, halves - 2, along) + PREDICT_TWO * (
        segment(updated, 0, halves - 3, along) + segment(updated, 1, halves - 2, along)
    )
    smoothed = segment(updated, 1, halves - 3, along) + UPDATE_TWO * (
        segment(refined, 0, halves - 4, along) + segment(refined, 1, halves - 3, along)
    )
    lowpass = smoothed * SCALE_LOW
    highpass = segment(refined, 1, halves - 3, along) * SCALE_HIGH
    paired = jnp.stack([lowpass, highpass], axis=along + 1)
    shape = list(extended.shape)
    shape[along] = length - 8
    return paired.reshape(shape)


def mirror(extended, along, at_start, at_end, margin):
    length = extended.shape[along]
    front = jnp.flip(segment(extended, margin + 1, 2 * margin + 1, along), along)
    behind = jnp.flip(segment(extended, length - 2 * margin - 1, length - margin - 1, along), along)
    head = jnp.where(at_start, front, segment(extended, 0, margin, along))
    tail = jnp.where(at_end, behind, segment(extended, length - margin, length, along))
    return jnp.concatenate(
        [head, segment(extended, margin, length - margin, along), tail], axis=along
    )


def shards(images):
    row_start = lax.axis_index("row") == 0
    row_end = lax.axis_index("row") == lax.axis_size("row") - 1
    col_start = lax.axis_index("col") == 0
    col_end = lax.axis_index("col") == lax.axis_size("col") - 1
    results = []
    lowband = images
    for level_index in range(LEVELS):
        extended = with_halo(lowband, (("row", 1), ("col", 2)), 4)
        extended = mirror(extended, 1, row_start, row_end, 4)
        extended = mirror(extended, 2, col_start, col_end, 4)
        vertical = lifting(extended, 1)
        transformed = lifting(vertical, 2)
        results.append(transformed)
        lowband = transformed[:, ::2, ::2]
    combined = results[-1]
    for transformed in reversed(results[:-1]):
        combined = transformed.at[:, ::2, ::2].set(combined)
    return combined


def solution(mesh):
    return jax.shard_map(
        shards,
        mesh=mesh,
        in_specs=(P(None, "row", "col"),),
        out_specs=P(None, "row", "col"),
        check_vma=False,
    )
```

profile of v0, /device:TPU:30, one launch (start us, length us, event | category | flops | bytes accessed | tf_op | source)
XLA Modules:
  0.0 318.5 jit_solution(421894064387704448)
XLA Ops:
  3.1 3.6 %collective-permute-start.1 = (f32[4,4,2048]{2,1,0:T(4,128)S(1)}, f32[4,4,2048]{2,1,0:T(4,128)S(1)}, u32[]{:S(2)}, u32[]{:S(2)}) collective-permute-start(f32[4,4,2048]{2,1,0:T(4,128)S(1)} %get-tuple-element.20), channel_id=1, source_target_pairs={{32,0},{64,32},{96,64},{128,96},{160,128},{192,160},{224,192},{33,... | collective-permute-start | bytes 393224 | tf_op jit(solution)/shard_map/ppermute | solution.py:25
  10.6 8.0 %collective-permute-start.3 = (f32[4,40,4]{2,1,0:T(8,128)S(1)}, f32[4,40,4]{2,1,0:T(8,128)S(1)}, u32[]{:S(2)}, u32[]{:S(2)}) collective-permute-start(f32[4,40,4]{2,1,0:T(8,128)S(1)} %get-tuple-element.15), channel_id=1, source_target_pairs={{1,0},{2,1},{3,2},{4,3},{5,4},{6,5},{7,6},{8,7},{9,8},{10,9},{11,1... | collective-permute-start | bytes 7688 | tf_op jit(solution)/shard_map/ppermute | solution.py:25
  20.7 6.4 %collective-permute-done.2 = f32[4,40,4]{2,1,0:T(8,128)S(1)} collective-permute-done((f32[4,40,4]{2,1,0:T(8,128)S(1)}, f32[4,40,4]{2,1,0:T(8,128)S(1)}, u32[]{:S(2)}, u32[]{:S(2)}) %collective-permute-start.2) | collective-permute-done | bytes 2592 | tf_op jit(solution)/shard_map/ppermute | solution.py:22
  39.7 18.2 %slice.418 = f32[4,32,1028]{2,0,1:T(4,128)S(1)} slice(f32[4,32,2056]{2,0,1:T(4,128)S(1)} %bitcast.55), slice={[0:4:1], [0:32:1], [0:2056:2]} | slice | bytes 1052672 | tf_op jit(solution)/shard_map/slice | solution.py:37
  57.9 18.2 %slice.420 = f32[4,32,1028]{2,0,1:T(4,128)S(1)} slice(f32[4,32,2056]{2,0,1:T(4,128)S(1)} %bitcast.56), slice={[0:4:1], [0:32:1], [1:2056:2]} | slice | bytes 1052672 | tf_op jit(solution)/shard_map/slice | solution.py:38
  78.8 4.5 %copy.56 = f32[4,32,1024,2]{1,3,2,0:T(2,128)} copy(f32[4,32,1024,2]{2,0,1,3:T(4,128)S(1)} %pad_maximum_fusion.3) | data formatting | bytes 2097152 | tf_op jit(solution)/shard_map/stack | solution.py:53
  83.3 15.6 %slice.432 = f32[4,16,1024]{1,2,0:T(8,128)S(1)} slice(f32[4,32,2048]{1,2,0:T(8,128)} %bitcast.54), slice={[0:4:1], [0:32:2], [0:2048:2]} | slice | bytes 524288 | tf_op jit(solution)/shard_map/slice | solution.py:84
  98.9 2.6 fusion.74
  103.7 2.9 copy.58
  106.6 3.0 collective-permute-start.5
  112.0 3.2 collective-permute-done.4
  118.3 3.9 %collective-permute-start.6 = (f32[4,24,4]{2,1,0:T(8,128)S(1)}, f32[4,24,4]{2,1,0:T(8,128)S(1)}, u32[]{:S(2)}, u32[]{:S(2)}) collective-permute-start(f32[4,24,4]{2,1,0:T(8,128)S(1)} %get-tuple-element.34), channel_id=1, source_target_pairs={{0,1},{1,2},{2,3},{3,4},{4,5},{5,6},{6,7},{7,8},{8,9},{9,10},{10,1... | collective-permute-start | bytes 4616 | tf_op jit(solution)/shard_map/ppermute | solution.py:22
  122.4 4.0 %collective-permute-done.6 = f32[4,24,4]{2,1,0:T(8,128)S(1)} collective-permute-done((f32[4,24,4]{2,1,0:T(8,128)S(1)}, f32[4,24,4]{2,1,0:T(8,128)S(1)}, u32[]{:S(2)}, u32[]{:S(2)}) %collective-permute-start.6) | collective-permute-done | bytes 1568 | tf_op jit(solution)/shard_map/ppermute | solution.py:22
  129.1 5.4 %slice.461 = f32[4,16,516]{2,0,1:T(4,128)S(1)} slice(f32[4,16,1032]{2,0,1:T(4,128)S(1)} %bitcast.60), slice={[0:4:1], [0:16:1], [0:1032:2]} | slice | bytes 264192 | tf_op jit(solution)/shard_map/slice | solution.py:37
  134.5 5.5 %slice.463 = f32[4,16,516]{2,0,1:T(4,128)S(1)} slice(f32[4,16,1032]{2,0,1:T(4,128)S(1)} %bitcast.61), slice={[0:4:1], [0:16:1], [1:1032:2]} | slice | bytes 264192 | tf_op jit(solution)/shard_map/slice | solution.py:38
  143.2 7.7 %slice.475 = f32[4,8,512]{1,2,0:T(8,128)S(1)} slice(f32[4,16,1024]{1,2,0:T(8,128)} %bitcast.57), slice={[0:4:1], [0:16:2], [0:1024:2]} | slice | bytes 131072 | tf_op jit(solution)/shard_map/slice | solution.py:84
  159.5 2.4 collective-permute-done.8
  164.0 6.3 %collective-permute-start.11 = (f32[4,16,4]{2,1,0:T(8,128)S(1)}, f32[4,16,4]{2,1,0:T(8,128)S(1)}, u32[]{:S(2)}, u32[]{:S(2)}) collective-permute-start(f32[4,16,4]{2,1,0:T(8,128)S(1)} %get-tuple-element.48), channel_id=1, source_target_pairs={{1,0},{2,1},{3,2},{4,3},{5,4},{6,5},{7,6},{8,7},{9,8},{10,9},{11,1... | collective-permute-start | bytes 3080 | tf_op jit(solution)/shard_map/ppermute | solution.py:25
  170.3 31.4 %copy.55 = f32[4,32,1024,2]{0,3,2,1:T(2,128)} copy(f32[4,32,1024,2]{2,0,1,3:T(4,128)S(1)} %pad_maximum_fusion.3) | data formatting | bytes 2097152 | tf_op jit(solution)/shard_map/stack | solution.py:53
  201.7 8.5 %copy.61 = f32[4,16,512,2]{0,3,2,1:T(2,128)} copy(f32[4,16,512,2]{2,0,1,3:T(4,128)S(1)} %pad_maximum_fusion.7) | data formatting | bytes 524288 | tf_op jit(solution)/shard_map/stack | solution.py:53
  215.2 3.1 copy.71
  218.3 17.2 %scatter_fusion = f32[4,16384]{0,1:T(8,128)} fusion(f32[4,16384]{0,1:T(8,128)} %bitcast.53, s32[4096]{0:T(1024)S(1)} %bitcast.64, f32[4096,4]{1,0:T(8,128)S(1)} %bitcast.59), kind=kCustom, calls=%fused_computation | custom fusion | bytes 212992
  235.5 62.8 %scatter_custom_fusion.1 = f32[4,65536]{0,1:T(8,128)} fusion(f32[4,65536]{0,1:T(8,128)} %bitcast.51, s32[16384]{0:T(1024)S(1)} %bitcast.65, f32[4,16384]{0,1:T(8,128)} %scatter_fusion), kind=kCustom, calls=%fused_computation.2 | custom fusion | bytes 9437184
  298.2 20.3 %copy.70 = f32[4,32,2048]{2,1,0:T(8,128)} copy(f32[4,32,2048]{0,2,1:T(8,128)} %bitcast.52) | data formatting | bytes 2097152 | tf_op jit(solution)/shard_map/scatter | solution.py:87
  (149 shorter events, 53.0 us)
Async XLA Ops:
  0.0 9.2 %copy-start.6 = (f32[4,32,2048]{2,1,0:T(8,128)S(1)}, f32[4,32,2048]{2,1,0:T(8,128)}, u32[]{:S(2)}) copy-start(f32[4,32,2048]{2,1,0:T(8,128)} %param.1) | copy-start | bytes 3145732
  1.2 7.8 %collective-permute-start = (f32[4,4,2048]{2,1,0:T(4,128)S(1)}, f32[4,4,2048]{2,1,0:T(4,128)S(1)}, u32[]{:S(2)}, u32[]{:S(2)}) collective-permute-start(f32[4,4,2048]{2,1,0:T(4,128)S(1)} %get-tuple-element.19), channel_id=1, source_target_pairs={{0,32},{32,64},{64,96},{96,128},{128,160},{160,192},{192,224},{1,3... | collective-permute-start | bytes 393224 | tf_op jit(solution)/shard_map/ppermute | solution.py:22
  3.1 6.1 %collective-permute-start.1 = (f32[4,4,2048]{2,1,0:T(4,128)S(1)}, f32[4,4,2048]{2,1,0:T(4,128)S(1)}, u32[]{:S(2)}, u32[]{:S(2)}) collective-permute-start(f32[4,4,2048]{2,1,0:T(4,128)S(1)} %get-tuple-element.20), channel_id=1, source_target_pairs={{32,0},{64,32},{96,64},{128,96},{160,128},{192,160},{224,192},{33,... | collective-permute-start | bytes 393224 | tf_op jit(solution)/shard_map/ppermute | solution.py:25
  9.4 1.1 copy-start
  10.6 10.1 %collective-permute-start.3 = (f32[4,40,4]{2,1,0:T(8,128)S(1)}, f32[4,40,4]{2,1,0:T(8,128)S(1)}, u32[]{:S(2)}, u32[]{:S(2)}) collective-permute-start(f32[4,40,4]{2,1,0:T(8,128)S(1)} %get-tuple-element.15), channel_id=1, source_target_pairs={{1,0},{2,1},{3,2},{4,3},{5,4},{6,5},{7,6},{8,7},{9,8},{10,9},{11,1... | collective-permute-start | bytes 7688 | tf_op jit(solution)/shard_map/ppermute | solution.py:25
  18.6 8.4 %collective-permute-start.2 = (f32[4,40,4]{2,1,0:T(8,128)S(1)}, f32[4,40,4]{2,1,0:T(8,128)S(1)}, u32[]{:S(2)}, u32[]{:S(2)}) collective-permute-start(f32[4,40,4]{2,1,0:T(8,128)S(1)} %get-tuple-element.16), channel_id=1, source_target_pairs={{0,1},{1,2},{2,3},{3,4},{4,5},{5,6},{6,7},{7,8},{8,9},{9,10},{10,1... | collective-permute-start | bytes 7688 | tf_op jit(solution)/shard_map/ppermute | solution.py:22
  30.4 0.6 copy-start.2
  30.5 0.7 copy-start.4
  32.6 1.5 copy-start.3
  32.6 1.5 copy-start.5
  32.6 1.5 copy-start.7
  32.6 1.5 copy-start.8
  34.1 1.4 copy-start.1
  106.6 5.5 %collective-permute-start.5 = (f32[4,4,1024]{2,1,0:T(4,128)}, f32[4,4,1024]{2,1,0:T(4,128)S(1)}, u32[]{:S(2)}, u32[]{:S(2)}) collective-permute-start(f32[4,4,1024]{2,1,0:T(4,128)} %copy.58), channel_id=1, source_target_pairs={{32,0},{64,32},{96,64},{128,96},{160,128},{192,160},{224,192},{33,... | collective-permute-start | bytes 196616 | tf_op jit(solution)/shard_map/ppermute | solution.py:25
  109.5 5.7 %collective-permute-start.4 = (f32[4,4,1024]{2,1,0:T(4,128)S(1)}, f32[4,4,1024]{2,1,0:T(4,128)}, u32[]{:S(2)}, u32[]{:S(2)}) collective-permute-start(f32[4,4,1024]{2,1,0:T(4,128)S(1)} %copy.57), channel_id=1, source_target_pairs={{0,32},{32,64},{64,96},{96,128},{128,160},{160,192},{192,224},{1,3... | collective-permute-start | bytes 196616 | tf_op jit(solution)/shard_map/ppermute | solution.py:22
  111.5 10.8 %copy-start.11 = (s32[2]{0:T(128)S(1)}, s32[2]{0:T(128)}, u32[]{:S(2)}) copy-start(s32[2]{0:T(128)} %constant.6) | copy-start | bytes 28
  116.2 6.2 %collective-permute-start.7 = (f32[4,24,4]{2,1,0:T(8,128)S(1)}, f32[4,24,4]{2,1,0:T(8,128)S(1)}, u32[]{:S(2)}, u32[]{:S(2)}) collective-permute-start(f32[4,24,4]{2,1,0:T(8,128)S(1)} %get-tuple-element.33), channel_id=1, source_target_pairs={{1,0},{2,1},{3,2},{4,3},{5,4},{6,5},{7,6},{8,7},{9,8},{10,9},{11,1... | collective-permute-start | bytes 4616 | tf_op jit(solution)/shard_map/ppermute | solution.py:25
  118.3 8.1 %collective-permute-start.6 = (f32[4,24,4]{2,1,0:T(8,128)S(1)}, f32[4,24,4]{2,1,0:T(8,128)S(1)}, u32[]{:S(2)}, u32[]{:S(2)}) collective-permute-start(f32[4,24,4]{2,1,0:T(8,128)S(1)} %get-tuple-element.34), channel_id=1, source_target_pairs={{0,1},{1,2},{2,3},{3,4},{4,5},{5,6},{6,7},{7,8},{8,9},{9,10},{10,1... | collective-permute-start | bytes 4616 | tf_op jit(solution)/shard_map/ppermute | solution.py:22
  152.3 6.9 %copy-start.10 = (s32[2]{0:T(128)S(1)}, s32[2]{0:T(128)}, u32[]{:S(2)}) copy-start(s32[2]{0:T(128)} %constant.3) | copy-start | bytes 28
  153.9 16.4 %copy-start.9 = (s32[2,8,8,128]{3,2,1,0:T(8,128)S(1)}, s32[2,8,8,128]{3,2,1,0:T(8,128)}, u32[]{:S(2)}) copy-start(s32[2,8,8,128]{3,2,1,0:T(8,128)} %select_bitcast_fusion) | copy-start | bytes 196612
  154.8 4.7 %collective-permute-start.9 = (f32[4,4,512]{2,1,0:T(4,128)}, f32[4,4,512]{2,1,0:T(4,128)S(1)}, u32[]{:S(2)}, u32[]{:S(2)}) collective-permute-start(f32[4,4,512]{2,1,0:T(4,128)} %copy.64), channel_id=1, source_target_pairs={{32,0},{64,32},{96,64},{128,96},{160,128},{192,160},{224,192},{33,... | collective-permute-start | bytes 98312 | tf_op jit(solution)/shard_map/ppermute | solution.py:25
  156.7 5.2 %collective-permute-start.8 = (f32[4,4,512]{2,1,0:T(4,128)S(1)}, f32[4,4,512]{2,1,0:T(4,128)S(1)}, u32[]{:S(2)}, u32[]{:S(2)}) collective-permute-start(f32[4,4,512]{2,1,0:T(4,128)S(1)} %copy.63), channel_id=1, source_target_pairs={{0,32},{32,64},{64,96},{96,128},{128,160},{160,192},{192,224},{1,3... | collective-permute-start | bytes 98312 | tf_op jit(solution)/shard_map/ppermute | solution.py:22
  162.1 48.2 %collective-permute-start.10 = (f32[4,16,4]{2,1,0:T(8,128)S(1)}, f32[4,16,4]{2,1,0:T(8,128)S(1)}, u32[]{:S(2)}, u32[]{:S(2)}) collective-permute-start(f32[4,16,4]{2,1,0:T(8,128)S(1)} %get-tuple-element.47), channel_id=1, source_target_pairs={{0,1},{1,2},{2,3},{3,4},{4,5},{5,6},{6,7},{7,8},{8,9},{9,10},{10,1... | collective-permute-start | bytes 3080 | tf_op jit(solution)/shard_map/ppermute | solution.py:22
  164.0 46.2 %collective-permute-start.11 = (f32[4,16,4]{2,1,0:T(8,128)S(1)}, f32[4,16,4]{2,1,0:T(8,128)S(1)}, u32[]{:S(2)}, u32[]{:S(2)}) collective-permute-start(f32[4,16,4]{2,1,0:T(8,128)S(1)} %get-tuple-element.48), channel_id=1, source_target_pairs={{1,0},{2,1},{3,2},{4,3},{5,4},{6,5},{7,6},{8,7},{9,8},{10,9},{11,1... | collective-permute-start | bytes 3080 | tf_op jit(solution)/shard_map/ppermute | solution.py:25
where the time goes:
time: 320 us; the launch traced here: 319 us
  local copies, waits for them, and re-layouts  252 us (79%)
  starting transfers between devices  38.9 us (12%)
  waiting for transfers between devices  16.4 us (5%)
  other arithmetic  10.5 us (3%)
    unnamed x28, local copies, waits for them, and re-layouts  82.1 us
    another operation x8, local copies, waits for them, and re-layouts, lifting(): paired = jnp.stack([lowpass, highpass], axis=along + 1)  47.8 us
    slice x6, local copies, waits for them, and re-layouts, lifting(): odds = lax.slice_in_dim(extended, 1, length, 2, along)  25.7 us
    slice x6, local copies, waits for them, and re-layouts, lifting(): evens = lax.slice_in_dim(extended, 0, length, 2, along)  25.6 us
    ppermute x6, starting transfers between devices, with_halo(): lax.ppermute(lax.slice_in_dim(block, 0, width, axis=dim), axis, backward)  24.9 us
    slice x4, local copies, waits for them, and re-layouts, shards(): lowband = transformed[:, ::2, ::2]  24.2 us
    scatter x1, local copies, waits for them, and re-layouts, shards(): combined = transformed.at[:, ::2, ::2].set(combined)  20.3 us
    ppermute x6, waiting for transfers between devices, with_halo(): lax.ppermute(lax.slice_in_dim(block, block.shape[dim] - width, None, axis...  16 us
  transfers between devices with their start and end apart: 12, of which 6 were waited for; matrix products, arithmetic and copies ran while one was open for 14% of the time, Pallas kernels for 0%

commit v1 on v0

v1 whole, which is shorter than its diff:
```python
import jax
import jax.numpy as jnp
from jax import lax
from jax.experimental import pallas as pl
from jax.experimental.pallas import tpu as pltpu
from jax.sharding import PartitionSpec as P

ALPHA = -1.586134342
BETA = -0.05298011854
GAMMA = 0.8829110762
DELTA = 0.4435068522
SCALE_HIGH = 1.230174105
SCALE_LOW = 1.0 / 1.230174105

IMAGES = 4
ROWS = 32
CHUNKS = 16
TILES = IMAGES * CHUNKS
LANES = 128
KINDS = ((0, 4, 8), (4, 2, 16), (6, 1, 32))


def _lift(x, left, right):
    s, d = x[0::2], x[1::2]
    m = len(s)
    d = [d[i] + ALPHA * (s[i] + (s[i + 1] if i + 1 < m else right[0])) for i in range(m)]
    s = [s[i] + BETA * ((d[i - 1] if i else left[0]) + d[i]) for i in range(m)]
    d = [d[i] + GAMMA * (s[i] + (s[i + 1] if i + 1 < m else right[1])) for i in range(m)]
    s = [s[i] + DELTA * ((d[i - 1] if i else left[1]) + d[i]) for i in range(m)]
    return [v * SCALE_LOW for v in s]


def _states(x):
    p = x[-1] + ALPHA * x[-2]
    t = x[-2] + BETA * (x[-3] + ALPHA * (x[-4] + x[-2]))
    s = x[0]
    u = x[0] + BETA * (x[1] + ALPHA * (x[0] + x[2]))
    return p, t, s, u


def _responses():
    zero = (0.0, 0.0)
    end, start = {}, {}
    for level in (1, 2):
        for j in range(2):
            unit = (1.0, 0.0) if j == 0 else (0.0, 1.0)
            for table, left, right, pick in ((end, zero, unit, 0), (start, unit, zero, 2)):
                band = [0.0] * (ROWS >> (level - 1))
                low = _lift(band, left, right)
                for into in range(level + 1, 4):
                    table[level, into, j] = _states(low)[pick : pick + 2]
                    low = _lift(low, zero, zero)
    return end, start


END, START = _responses()


def _rows_of(ref, t):
    return [ref[t, pl.ds(q, 8, stride=4), :] for q in (0, 2, 1, 3)]


def _load_x(x_ref, scr, sems):
    copies = []
    for img in range(IMAGES):
        for rt in range(4):
            copies.append(
                pltpu.make_async_copy(
                    x_ref.at[img, rt],
                    scr.at[pl.ds(img * CHUNKS, CHUNKS), pl.ds(rt * 8, 8), :],
                    sems.at[img, rt],
                )
            )
    for c in copies:
        c.start()
    return copies


def _sub_iota():
    return lax.broadcasted_iota(jnp.int32, (8, LANES), 0)


def states_kernel(x_ref, down_ref, up_ref, scr, sems):
    copies = _load_x(x_ref, scr, sems)
    sub = _sub_iota()
    is7 = sub == 7
    is0 = sub == 0
    odd = (sub & 1) == 1
    zero = jnp.zeros((8, LANES), jnp.float32)

    def up(v):
        return jnp.where(is7, zero, pltpu.roll(v, 7, 0))

    def dn(v):
        return jnp.where(is0, zero, pltpu.roll(v, 1, 0))

    def body(t, carry):
        a, b, c, d = _rows_of(scr, t)
        lo, hi = [], []
        lo.append((d + ALPHA * b)[7:8])
        c1 = c + ALPHA * (a + b)
        lo.append((b + BETA * c1)[7:8])
        hi.append(a[0:1])
        hi.append((a + BETA * c1)[0:1])
        d1 = d + ALPHA * (b + up(a))
        a1 = a + BETA * (dn(d1) + c1)
        b1 = b + BETA * (c1 + d1)
        c2 = c1 + GAMMA * (a1 + b1)
        d2 = d1 + GAMMA * (b1 + up(a1))
        a = (a1 + DELTA * (dn(d2) + c2)) * SCALE_LOW
        b = (b1 + DELTA * (c2 + d2)) * SCALE_LOW
        lo.append((b + ALPHA * a)[7:8])
        b1 = b + ALPHA * (a + up(a))
        rb = dn(b1)
        lo.append((a + BETA * rb)[7:8])
        hi.append(a[0:1])
        hi.append((a + BETA * b1)[0:1])
        a1 = a + BETA * (rb + b1)
        b2 = b1 + GAMMA * (a1 + up(a1))
        x = (a1 + DELTA * (dn(b2) + b2)) * SCALE_LOW
        ru = pltpu.roll(x, 1, 0)
        lo.append((x + ALPHA * ru)[7:8])
        x1 = x + ALPHA * (ru + pltpu.roll(x, 7, 0))
        lo.append((x + BETA * pltpu.roll(x1, 1, 0))[6:7])
        hi.append(x[0:1])
        hi.append((x + BETA * pltpu.roll(x1, 7, 0))[0:1])
        for k in range(6):
            down_ref[pl.ds(k * TILES + t, 1), :] = lo[k]
            up_ref[pl.ds(k * TILES + t, 1), :] = hi[k]
        return carry

    for img in range(IMAGES):
        for rt in range(4):
            copies[img * 4 + rt].wait()
        lax.fori_loop(img * CHUNKS, (img + 1) * CHUNKS, body, 0)


def _boundary(k, ref):
    return ref[pl.ds(k * TILES, TILES), :]


def _junction(ends, starts):
    out = []
    for level in (1, 2, 3):
        p, t = ends[2 * level - 2], ends[2 * level - 1]
        s, u = starts[2 * level - 2], starts[2 * level - 1]
        for prior in range(1, level):
            l1, l2, r1, r2 = out[prior - 1]
            e0, e1 = END[prior, level, 0], END[prior, level, 1]
            s0, s1 = START[prior, level, 0], START[prior, level, 1]
            p = p + e0[0] * r1 + e1[0] * r2
            t = t + e0[1] * r1 + e1[1] * r2
            s = s + s0[0] * l1 + s1[0] * l2
            u = u + s0[1] * l1 + s1[1] * l2
        l1 = p + ALPHA * s
        r2 = u + BETA * l1
        l2 = l1 + GAMMA * (t + BETA * l1 + r2)
        out.append((l1, l2, s, r2))
    return out


def rows_kernel(x_ref, own_end, own_start, got_end, got_start, v_ref, left_ref, right_ref, scr, bnd, sems):
    copies = _load_x(x_ref, scr, sems)
    row = lax.axis_index("row")
    first = row == 0
    last = row == lax.axis_size("row") - 1
    top = _junction([_boundary(k, got_end) for k in range(6)], [_boundary(k, own_start) for k in range(6)])
    for level in range(3):
        for j in range(2):
            bnd[pl.ds((level * 4 + j) * TILES, TILES), :] = top[level][j]
    low = _junction([_boundary(k, own_end) for k in range(6)], [_boundary(k, got_start) for k in range(6)])
    for level in range(3):
        for j in range(2, 4):
            bnd[pl.ds((level * 4 + j) * TILES, TILES), :] = low[level][j]

    sub = _sub_iota()
    is7 = sub == 7
    is0 = sub == 0
    mir7 = is7 & last
    mir0 = is0 & first
    odd = (sub & 1) == 1
    zero = jnp.zeros((8, LANES), jnp.float32)
    c_alpha = jnp.where(odd, ALPHA, zero)
    c_beta = jnp.where(odd, zero, BETA)
    c_gamma = jnp.where(odd, GAMMA, zero)
    c_delta = jnp.where(odd, zero, DELTA)
    c_scale = jnp.where(odd, SCALE_HIGH, SCALE_LOW).astype(jnp.float32)

    def body(t, carry):
        def edge(level, j):
            return jnp.broadcast_to(bnd[pl.ds(((level - 1) * 4 + j) * TILES + t, 1), :], (8, LANES))

        def up(v, level, j, mirror):
            return jnp.where(mir7, mirror, jnp.where(is7, edge(level, j), pltpu.roll(v, 7, 0)))

        def dn(v, level, j, mirror):
            return jnp.where(mir0, mirror, jnp.where(is0, edge(level, j), pltpu.roll(v, 1, 0)))

        a, b, c, d = _rows_of(scr, t)
        c1 = c + ALPHA * (a + b)
        d1 = d + ALPHA * (b + up(a, 1, 2, b))
        a1 = a + BETA * (dn(d1, 1, 0, c1) + c1)
        b1 = b + BETA * (c1 + d1)
        c2 = c1 + GAMMA * (a1 + b1)
        d2 = d1 + GAMMA * (b1 + up(a1, 1, 3, b1))
        a = (a1 + DELTA * (dn(d2, 1, 1, c2) + c2)) * SCALE_LOW
        b = (b1 + DELTA * (c2 + d2)) * SCALE_LOW
        v_ref[t, 0] = a
        v_ref[t, 1] = b
        v_ref[t, 2] = c2 * SCALE_HIGH
        v_ref[t, 3] = d2 * SCALE_HIGH
        b1 = b + ALPHA * (a + up(a, 2, 2, a))
        a1 = a + BETA * (dn(b1, 2, 0, b1) + b1)
        b2 = b1 + GAMMA * (a1 + up(a1, 2, 3, a1))
        x = (a1 + DELTA * (dn(b2, 2, 1, b2) + b2)) * SCALE_LOW
        v_ref[t, 4] = x
        v_ref[t, 5] = b2 * SCALE_HIGH
        for co, ce, j in ((c_alpha, c_beta, 0), (c_gamma, c_delta, 1)):
            l = pltpu.roll(x, 1, 0)
            x = x + co * (l + up(x, 3, 2 + j, l))
            r = pltpu.roll(x, 7, 0)
            x = x + ce * (dn(x, 3, j, r) + r)
        v_ref[t, 6] = x * c_scale
        return carry

    for img in range(IMAGES):
        for rt in range(4):
            copies[img * 4 + rt].wait()
        lax.fori_loop(img * CHUNKS, (img + 1) * CHUNKS, body, 0)

    lane = lax.broadcasted_iota(jnp.int32, (8, LANES), 1)
    for n, (base, count, width) in enumerate(KINDS):
        to_left = zero
        to_right = zero
        for img in range(IMAGES):
            for q in range(count):
                slot = (img * count + q) * width
                here = (lane >= slot) & (lane < slot + width)
                start = v_ref[img * CHUNKS, base + q]
                end = v_ref[img * CHUNKS + CHUNKS - 1, base + q]
                if slot:
                    start = pltpu.roll(start, slot, 1)
                if (slot + width) % LANES:
                    end = pltpu.roll(end, slot + width, 1)
                to_left = jnp.where(here, start, to_left)
                to_right = jnp.where(here, end, to_right)
        left_ref[pl.ds(8 * n, 8), :] = to_left
        right_ref[pl.ds(8 * n, 8), :] = to_right


def cols_kernel(v_ref, from_left, from_right, out_ref, scr, halo, sems):
    col = lax.axis_index("col")
    first = col == 0
    last = col == lax.axis_size("col") - 1
    lane = lax.broadcasted_iota(jnp.int32, (8, LANES), 1)
    zero = jnp.zeros((8, LANES), jnp.float32)

    for n, (base, count, width) in enumerate(KINDS):
        got_l = from_left[pl.ds(8 * n, 8), :]
        got_r = from_right[pl.ds(8 * n, 8), :]
        for img in range(IMAGES):
            for q in range(count):
                slot = (img * count + q) * width
                halo[img, base + q, 0] = pltpu.roll(got_l, (LANES - slot - width) % LANES, 1) if (slot + width) % LANES else got_l
                halo[img, base + q, 1] = pltpu.roll(got_r, (LANES - slot) % LANES, 1) if slot else got_r

    def level_pass(xs, level):
        st = 1 << (level - 1)
        pos = lane & (2 * st - 1)
        co = pos == st
        ce = pos == 0
        hi_edge = lane >= LANES - st
        lo_edge = lane < st
        mir_hi = hi_edge & last
        mir_lo = lo_edge & first
        n = len(xs)
        for ka, kb in ((ALPHA, BETA), (GAMMA, DELTA)):
            ca = jnp.where(co, ka, zero)
            cb = jnp.where(ce, kb, zero)
            rights = [pltpu.roll(x, LANES - st, 1) for x in xs]
            lefts = [pltpu.roll(x, st, 1) for x in xs]
            new = []
            for i in range(n):
                r = rights[i]
                if i + 1 < n:
                    r = jnp.where(hi_edge, rights[i + 1], r)
                if i == n - 2:
                    r = jnp.where(mir_hi, lefts[i], r)
                new.append(xs[i] + ca * (lefts[i] + r))
            xs = new
            rights = [pltpu.roll(x, LANES - st, 1) for x in xs]
            lefts = [pltpu.roll(x, st, 1) for x in xs]
            new = []
            for i in range(n):
                l = lefts[i]
                if i:
                    l = jnp.where(lo_edge, lefts[i - 1], l)
                if i == 1:
                    l = jnp.where(mir_lo, rights[i], l)
                new.append(xs[i] + cb * (l + rights[i]))
            xs = new
        scale = jnp.where(co, SCALE_HIGH, SCALE_LOW).astype(jnp.float32)
        return [x * scale for x in xs]

    def line(img, k):
        return (
            [halo[img, k, 0]]
            + [v_ref[img * CHUNKS + c, k] for c in range(CHUNKS)]
            + [halo[img, k, 1]]
        )

    def put(img, q, keep, xs):
        for c in range(CHUNKS):
            where = (img * CHUNKS + c, pl.ds((q & 1) * 2 + (q >> 1), 8, stride=4), slice(None))
            val = xs[c + 1]
            if keep is not None:
                val = jnp.where(keep, val, scr[where])
            scr[where] = val

    def image(img, carry):
        def v1(q, carry):
            put(img, q, None, level_pass(line(img, q), 1))
            return carry

        lax.fori_loop(0, 4, v1, 0)

        def v2(q, carry):
            put(img, q, (lane & 1) == 0, level_pass(level_pass(line(img, 4 + q), 1), 2))
            return carry

        lax.fori_loop(0, 2, v2, 0)
        xs = line(img, 6)
        for level in (1, 2, 3):
            xs = level_pass(xs, level)
        put(img, 0, (lane & 3) == 0, xs)
        for rt in range(4):
            pltpu.make_async_copy(
                scr.at[pl.ds(img * CHUNKS, CHUNKS), pl.ds(rt * 8, 8), :], out_ref.at[img, rt], sems.at[img, rt]
            ).start()
        return carry

    for img in range(IMAGES):
        image(img, 0)
    for img in range(IMAGES):
        for rt in range(4):
            pltpu.make_async_copy(
                scr.at[pl.ds(img * CHUNKS, CHUNKS), pl.ds(rt * 8, 8), :], out_ref.at[img, rt], sems.at[img, rt]
            ).wait()


def _swaps(count):
    even = [(i, i ^ 1) for i in range(count)]
    odd = [(i, i + 1 if i % 2 else i - 1) for i in range(1, count - 1)] + [(0, count - 1), (count - 1, 0)]
    return even, odd


def exchange(axis, to_prev, to_next):
    even_pairs, odd_pairs = _swaps(lax.axis_size(axis))
    is_odd = lax.axis_index(axis) % 2 == 1
    via_even = lax.ppermute(jnp.where(is_odd, to_prev, to_next), axis, even_pairs)
    via_odd = lax.ppermute(jnp.where(is_odd, to_next, to_prev), axis, odd_pairs)
    from_prev = jnp.where(is_odd, via_even, via_odd)
    from_next = jnp.where(is_odd, via_odd, via_even)
    return from_prev, from_next


F32 = jnp.float32
VMEM = pl.BlockSpec(memory_space=pltpu.VMEM)
ANY = pl.BlockSpec(memory_space=pl.ANY)


def shards(images):
    x = images.reshape(IMAGES, 4, 8, CHUNKS, LANES).transpose(0, 1, 3, 2, 4)
    state = jax.ShapeDtypeStruct((6 * TILES, LANES), F32)
    end, start = pl.pallas_call(
        states_kernel,
        out_shape=(state, state),
        in_specs=[ANY],
        out_specs=(VMEM, VMEM),
        scratch_shapes=[pltpu.VMEM((TILES, ROWS, LANES), F32), pltpu.SemaphoreType.DMA((IMAGES, 4))],
        name="row_states",
    )(x)
    got_end, got_start = exchange("row", start, end)
    edge = jax.ShapeDtypeStruct((24, LANES), F32)
    v, to_left, to_right = pl.pallas_call(
        rows_kernel,
        out_shape=(jax.ShapeDtypeStruct((TILES, 7, 8, LANES), F32), edge, edge),
        in_specs=[ANY, VMEM, VMEM, VMEM, VMEM],
        out_specs=(VMEM, VMEM, VMEM),
        scratch_shapes=[
            pltpu.VMEM((TILES, ROWS, LANES), F32),
            pltpu.VMEM((12 * TILES, LANES), F32),
            pltpu.SemaphoreType.DMA((IMAGES, 4)),
        ],
        name="rows_all",
    )(x, end, start, got_end, got_start)
    from_left, from_right = exchange("col", to_left, to_right)
    out = pl.pallas_call(
        cols_kernel,
        out_shape=jax.ShapeDtypeStruct((IMAGES, 4, CHUNKS, 8, LANES), F32),
        in_specs=[VMEM, VMEM, VMEM],
        out_specs=ANY,
        scratch_shapes=[
            pltpu.VMEM((TILES, ROWS, LANES), F32),
            pltpu.VMEM((IMAGES, 7, 2, 8, LANES), F32),
            pltpu.SemaphoreType.DMA((IMAGES, 4)),
        ],
        name="cols_all",
    )(v, from_left, from_right)
    return out.transpose(0, 1, 3, 2, 4).reshape(IMAGES, ROWS, CHUNKS * LANES)


def solution(mesh):
    return jax.shard_map(
        shards,
        mesh=mesh,
        in_specs=(P(None, "row", "col"),),
        out_specs=P(None, "row", "col"),
        check_vma=False,
    )
```

time: 320 us -> 52.3 us (0.16)
  the two profiles are of different devices: /device:TPU:30 before, /device:TPU:1 now
where the time goes in v1:
time: 52.3 us; the launch traced here: 52 us
  Pallas kernels  31.8 us (61%)
  starting transfers between devices  12.1 us (23%)
  waiting for transfers between devices  4.92 us (9%)
  other arithmetic  3.15 us (6%)
    pallas_call x1, Pallas kernels, shards(): pl.pallas_call(cols_kernel, out_shape=jax.ShapeDtypeStruct((IMAGES, 4, CH...  19 us
    ppermute x2, starting transfers between devices, exchange(): via_odd = lax.ppermute(jnp.where(is_odd, to_next, to_prev), axis, odd_pairs)  10.8 us
    pallas_call x1, Pallas kernels, shards(): pl.pallas_call(rows_kernel, out_shape=(jax.ShapeDtypeStruct((TILES, 7, 8,...  7.92 us
    pallas_call x1, Pallas kernels, shards(): pl.pallas_call(states_kernel, out_shape=(state, state), in_specs=[ANY], o...  4.93 us
    ppermute x2, waiting for transfers between devices, exchange(): via_odd = lax.ppermute(jnp.where(is_odd, to_next, to_prev), axis, odd_pairs)  3.16 us
    select_n x2, other arithmetic, exchange(): via_odd = lax.ppermute(jnp.where(is_odd, to_next, to_prev), axis, odd_pairs)  1.78 us
    ppermute x2, waiting for transfers between devices, exchange(): lax.ppermute(jnp.where(is_odd, to_prev, to_next), axis, even_pairs)  1.76 us
    select_n x2, other arithmetic, exchange(): from_next = jnp.where(is_odd, via_odd, via_even)  1.37 us
  transfers between devices with their start and end apart: 4, of which 3 were waited for; matrix products, arithmetic and copies ran while one was open for 0% of the time, Pallas kernels for 0%

profile of v1, /device:TPU:1, one launch (start us, length us, event | category | flops | bytes accessed | tf_op | source)
XLA Modules:
  0.0 52.0 jit_solution(15247963149424040383)
XLA Ops:
  0.0 4.9 %row_states.1 = (f32[384,128]{1,0:T(8,128)}, f32[384,128]{1,0:T(8,128)}) custom-call(f32[4,4,16,8,128]{4,3,2,1,0:T(8,128)} %bitcast.6), custom_call_target="tpu_custom_call" | custom-call | tf_op jit(solution)/shard_map/row_states/pallas_call | solution.py:375
  4.9 1.1 %broadcast_select_fusion.2 = (f32[384,128]{1,0:T(8,128)S(1)}, f32[384,128]{1,0:T(8,128)S(1)}) fusion(f32[384,128]{1,0:T(8,128)} %get-tuple-element.10.own_end, f32[384,128]{1,0:T(8,128)} %get-tuple-element.11.own_start, pred[]{:T(512)S(6)} %eq.9), kind=kLoop, calls=%fused_computation.2 | loop fusion | flops 98304 | bytes 786433 | tf_op jit(solution)/shard_map/jit(_where)/select_n | solution.py:361
  6.0 2.8 %collective-permute-start.1 = (f32[384,128]{1,0:T(8,128)S(1)}, f32[384,128]{1,0:T(8,128)S(1)}, u32[]{:S(2)}, u32[]{:S(2)}) collective-permute-start(f32[384,128]{1,0:T(8,128)S(1)} %get-tuple-element.17), channel_id=1, source_target_pairs={{32,64},{64,32},{96,128},{128,96},{160,192},{192,160},{0,224},{224... | collective-permute-start | bytes 589832 | tf_op jit(solution)/shard_map/ppermute | solution.py:361
  8.8 1.3 %collective-permute-start = (f32[384,128]{1,0:T(8,128)S(1)}, f32[384,128]{1,0:T(8,128)S(1)}, u32[]{:S(2)}, u32[]{:S(2)}) collective-permute-start(f32[384,128]{1,0:T(8,128)S(1)} %get-tuple-element.18), channel_id=1, source_target_pairs={{0,32},{32,0},{64,96},{96,64},{128,160},{160,128},{192,224},{224,1... | collective-permute-start | bytes 589832 | tf_op jit(solution)/shard_map/ppermute | solution.py:360
  10.0 2.1 %collective-permute-done.1 = f32[384,128]{1,0:T(8,128)S(1)} collective-permute-done((f32[384,128]{1,0:T(8,128)S(1)}, f32[384,128]{1,0:T(8,128)S(1)}, u32[]{:S(2)}, u32[]{:S(2)}) %collective-permute-start.1) | collective-permute-done | bytes 196640 | tf_op jit(solution)/shard_map/ppermute | solution.py:361
  12.1 0.0 collective-permute-done
  12.1 0.8 %broadcast_select_fusion = (f32[384,128]{1,0:T(8,128)}, f32[384,128]{1,0:T(8,128)}) fusion(f32[384,128]{1,0:T(8,128)S(1)} %collective-permute-done.1, f32[384,128]{1,0:T(8,128)S(1)} %collective-permute-done, pred[]{:T(512)S(6)} %eq.9), kind=kLoop, calls=%fused_computation | loop fusion | flops 98304 | bytes 786433 | tf_op jit(solution)/shard_map/jit(_where)/select_n | solution.py:363
  12.9 7.9 %rows_all.1 = (f32[64,7,8,128]{3,2,1,0:T(8,128)}, f32[24,128]{1,0:T(8,128)}, f32[24,128]{1,0:T(8,128)}) custom-call(f32[4,4,16,8,128]{4,3,2,1,0:T(8,128)} %bitcast.7, f32[384,128]{1,0:T(8,128)} %get-tuple-element.10.own_end, f32[384,128]{1,0:T(8,128)} %get-tuple-element.11.own_start, f32[384,128]{1,0:T(8,128)} %get-tuple-element.16.got_end, ...), custom_call_target="tpu_custom_call" | custom-call | tf_op jit(solution)/shard_map/rows_all/pallas_call | solution.py:385
  20.8 0.7 %broadcast_select_fusion.6 = (f32[24,128]{1,0:T(8,128)S(1)}, f32[24,128]{1,0:T(8,128)S(1)}) fusion(f32[24,128]{1,0:T(8,128)} %get-tuple-element.14, f32[24,128]{1,0:T(8,128)} %get-tuple-element.13, pred[]{:T(512)S(6)} %eq.10), kind=kLoop, calls=%fused_computation.6 | loop fusion | flops 6144 | bytes 49153 | tf_op jit(solution)/shard_map/jit(_where)/select_n | solution.py:361
  21.5 8.1 %collective-permute-start.3 = (f32[24,128]{1,0:T(8,128)S(1)}, f32[24,128]{1,0:T(8,128)S(1)}, u32[]{:S(2)}, u32[]{:S(2)}) collective-permute-start(f32[24,128]{1,0:T(8,128)S(1)} %get-tuple-element.21), channel_id=1, source_target_pairs={{1,2},{2,1},{3,4},{4,3},{5,6},{6,5},{7,8},{8,7},{9,10},{10,9},{11,... | collective-permute-start | bytes 36872 | tf_op jit(solution)/shard_map/ppermute | solution.py:361
  29.6 0.0 collective-permute-start.2
  29.6 1.1 %collective-permute-done.3 = f32[24,128]{1,0:T(8,128)S(1)} collective-permute-done((f32[24,128]{1,0:T(8,128)S(1)}, f32[24,128]{1,0:T(8,128)S(1)}, u32[]{:S(2)}, u32[]{:S(2)}) %collective-permute-start.3) | collective-permute-done | bytes 12320 | tf_op jit(solution)/shard_map/ppermute | solution.py:361
  30.7 1.8 %collective-permute-done.2 = f32[24,128]{1,0:T(8,128)S(1)} collective-permute-done((f32[24,128]{1,0:T(8,128)S(1)}, f32[24,128]{1,0:T(8,128)S(1)}, u32[]{:S(2)}, u32[]{:S(2)}) %collective-permute-start.2) | collective-permute-done | bytes 12320 | tf_op jit(solution)/shard_map/ppermute | solution.py:360
  32.4 0.6 %broadcast_select_fusion.4 = (f32[24,128]{1,0:T(8,128)}, f32[24,128]{1,0:T(8,128)}) fusion(f32[24,128]{1,0:T(8,128)S(1)} %collective-permute-done.3, f32[24,128]{1,0:T(8,128)S(1)} %collective-permute-done.2, pred[]{:T(512)S(6)} %eq.10), kind=kLoop, calls=%fused_computation.4 | loop fusion | flops 6144 | bytes 49153 | tf_op jit(solution)/shard_map/jit(_where)/select_n | solution.py:363
  33.1 19.0 %cols_all.1 = f32[4,4,16,8,128]{4,3,2,1,0:T(8,128)} custom-call(f32[64,7,8,128]{3,2,1,0:T(8,128)} %get-tuple-element.12.v_ref, f32[24,128]{1,0:T(8,128)} %get-tuple-element.20.from_left, f32[24,128]{1,0:T(8,128)} %get-tuple-element.19.from_right), custom_call_target="tpu_custom_call" | custom-call | tf_op jit(solution)/shard_map/cols_all/pallas_call | solution.py:398
Async XLA Ops:
  6.0 6.1 %collective-permute-start.1 = (f32[384,128]{1,0:T(8,128)S(1)}, f32[384,128]{1,0:T(8,128)S(1)}, u32[]{:S(2)}, u32[]{:S(2)}) collective-permute-start(f32[384,128]{1,0:T(8,128)S(1)} %get-tuple-element.17), channel_id=1, source_target_pairs={{32,64},{64,32},{96,128},{128,96},{160,192},{192,160},{0,224},{224... | collective-permute-start | bytes 589832 | tf_op jit(solution)/shard_map/ppermute | solution.py:361
  8.8 3.4 %collective-permute-start = (f32[384,128]{1,0:T(8,128)S(1)}, f32[384,128]{1,0:T(8,128)S(1)}, u32[]{:S(2)}, u32[]{:S(2)}) collective-permute-start(f32[384,128]{1,0:T(8,128)S(1)} %get-tuple-element.18), channel_id=1, source_target_pairs={{0,32},{32,0},{64,96},{96,64},{128,160},{160,128},{192,224},{224,1... | collective-permute-start | bytes 589832 | tf_op jit(solution)/shard_map/ppermute | solution.py:360
  21.5 9.1 %collective-permute-start.3 = (f32[24,128]{1,0:T(8,128)S(1)}, f32[24,128]{1,0:T(8,128)S(1)}, u32[]{:S(2)}, u32[]{:S(2)}) collective-permute-start(f32[24,128]{1,0:T(8,128)S(1)} %get-tuple-element.21), channel_id=1, source_target_pairs={{1,2},{2,1},{3,4},{4,3},{5,6},{6,5},{7,8},{8,7},{9,10},{10,9},{11,... | collective-permute-start | bytes 36872 | tf_op jit(solution)/shard_map/ppermute | solution.py:361
  29.6 2.8 %collective-permute-start.2 = (f32[24,128]{1,0:T(8,128)S(1)}, f32[24,128]{1,0:T(8,128)S(1)}, u32[]{:S(2)}, u32[]{:S(2)}) collective-permute-start(f32[24,128]{1,0:T(8,128)S(1)} %get-tuple-element.22), channel_id=1, source_target_pairs={{0,1},{1,0},{2,3},{3,2},{4,5},{5,4},{6,7},{7,6},{8,9},{9,8},{10,11... | collective-permute-start | bytes 36872 | tf_op jit(solution)/shard_map/ppermute | solution.py:360

commit v2 on v0

v2 whole, which is shorter than its diff:
```python
import jax
import jax.numpy as jnp
import numpy as np
from jax import lax
from jax.experimental import pallas as pl
from jax.experimental.pallas import tpu as pltpu
from jax.sharding import PartitionSpec as P

ALPHA = -1.586134342
BETA = -0.05298011854
GAMMA = 0.8829110762
DELTA = 0.4435068522
SCALE_HIGH = 1.230174105
SCALE_LOW = 1.0 / 1.230174105

IMAGES = 4
ROWS = 32
CHUNKS = 16
TILES = IMAGES * CHUNKS
LANES = 128
EDGES = 2 * IMAGES
HALF = LANES // 2
PATCH = 32
F32 = jnp.float32
OFFSETS = (0, 2, 1, 3)
KINDS = ((0, 4, 8), (4, 2, 16), (6, 1, 32))


def tile_row(img, chunk):
    place = 0 if chunk == 0 else 1 if chunk == CHUNKS - 1 else chunk + 1
    return place * IMAGES + img


def _lift(x, left, right):
    s, d = x[0::2], x[1::2]
    m = len(s)
    d = [d[i] + ALPHA * (s[i] + (s[i + 1] if i + 1 < m else right[0])) for i in range(m)]
    s = [s[i] + BETA * ((d[i - 1] if i else left[0]) + d[i]) for i in range(m)]
    d = [d[i] + GAMMA * (s[i] + (s[i + 1] if i + 1 < m else right[1])) for i in range(m)]
    s = [s[i] + DELTA * ((d[i - 1] if i else left[1]) + d[i]) for i in range(m)]
    return [v * SCALE_LOW for v in s], [v * SCALE_HIGH for v in d]


def _states(x):
    p = x[-1] + ALPHA * x[-2]
    t = x[-2] + BETA * (x[-3] + ALPHA * (x[-4] + x[-2]))
    s = x[0]
    u = x[0] + BETA * (x[1] + ALPHA * (x[0] + x[2]))
    return p, t, s, u


def _responses():
    zero = (0.0, 0.0)
    end, start = {}, {}
    for level in (1, 2):
        for j in range(2):
            unit = (1.0, 0.0) if j == 0 else (0.0, 1.0)
            for table, left, right, pick in ((end, zero, unit, 0), (start, unit, zero, 2)):
                band = [0.0] * (ROWS >> (level - 1))
                low, _ = _lift(band, left, right)
                for into in range(level + 1, 4):
                    table[level, into, j] = _states(low)[pick : pick + 2]
                    low, _ = _lift(low, zero, zero)
    return end, start


def _taps():
    low, high = [0.0] * 9, [0.0] * 9
    for k in range(-4, 5):
        x = [0.0] * 64
        x[32 + k] = 1.0
        low[k + 4] = _lift(x, (0.0, 0.0), (0.0, 0.0))[0][16]
        x = [0.0] * 64
        x[33 + k] = 1.0
        high[k + 4] = _lift(x, (0.0, 0.0), (0.0, 0.0))[1][16]
    return low, high


END, START = _responses()
LOW, HIGH = _taps()


def _edge_taps():
    table = np.zeros((2, 2, 3, 9, LANES), np.float32)
    for side in range(2):
        for mirrored in range(2):
            for level in range(3):
                st = 1 << level
                for lane in range(0, LANES, st):
                    taps = HIGH if (lane // st) % 2 else LOW
                    for k in range(-4, 5):
                        target = lane + k * st
                        if mirrored and side == 0 and target < HALF <= lane:
                            target = 2 * HALF - target
                        edge = HALF - st
                        if mirrored and side == 1 and target > edge >= lane:
                            target = 2 * edge - target
                        table[side, mirrored, level, (target - lane) // st + 4, lane] += taps[k + 4]
    return table.reshape(2 * 2, 27, LANES)


EDGE_TAPS = _edge_taps()


def _sub():
    return lax.broadcasted_iota(jnp.int32, (8, LANES), 0)


def _lane():
    return lax.broadcasted_iota(jnp.int32, (8, LANES), 1)


def _load(src, dst, sem):
    copy = pltpu.make_async_copy(src, dst, sem)
    copy.start()
    return copy


def _rows_of(ref, t):
    return [ref[t, pl.ds(q, 8, stride=4), :] for q in OFFSETS]


def _states_of(tile):
    sub = _sub()
    is7, is0 = sub == 7, sub == 0
    zero = jnp.zeros((8, LANES), F32)

    def up(v):
        return jnp.where(is7, zero, pltpu.roll(v, 7, 0))

    def dn(v):
        return jnp.where(is0, zero, pltpu.roll(v, 1, 0))

    a, b, c, d = tile
    c1 = c + ALPHA * (a + b)
    end = [(d + ALPHA * b)[7:8], (b + BETA * c1)[7:8]]
    start = [a[0:1], (a + BETA * c1)[0:1]]
    d1 = d + ALPHA * (b + up(a))
    a1 = a + BETA * (dn(d1) + c1)
    b1 = b + BETA * (c1 + d1)
    c2 = c1 + GAMMA * (a1 + b1)
    d2 = d1 + GAMMA * (b1 + up(a1))
    a = (a1 + DELTA * (dn(d2) + c2)) * SCALE_LOW
    b = (b1 + DELTA * (c2 + d2)) * SCALE_LOW
    b1 = b + ALPHA * (a + up(a))
    rb = dn(b1)
    end += [(b + ALPHA * a)[7:8], (a + BETA * rb)[7:8]]
    start += [a[0:1], (a + BETA * b1)[0:1]]
    a1 = a + BETA * (rb + b1)
    b2 = b1 + GAMMA * (a1 + up(a1))
    x = (a1 + DELTA * (dn(b2) + b2)) * SCALE_LOW
    back = pltpu.roll(x, 1, 0)
    x1 = x + ALPHA * (back + pltpu.roll(x, 7, 0))
    end += [(x + ALPHA * back)[7:8], (x + BETA * pltpu.roll(x1, 1, 0))[6:7]]
    start += [x[0:1], (x + BETA * pltpu.roll(x1, 7, 0))[0:1]]
    return end, start


def _junction(ends, starts):
    out = []
    for level in (1, 2, 3):
        p, t = ends[2 * level - 2], ends[2 * level - 1]
        s, u = starts[2 * level - 2], starts[2 * level - 1]
        for prior in range(1, level):
            l1, l2, r1, r2 = out[prior - 1]
            e0, e1 = END[prior, level, 0], END[prior, level, 1]
            s0, s1 = START[prior, level, 0], START[prior, level, 1]
            p = p + e0[0] * r1 + e1[0] * r2
            t = t + e0[1] * r1 + e1[1] * r2
            s = s + s0[0] * l1 + s1[0] * l2
            u = u + s0[1] * l1 + s1[1] * l2
        l1 = p + ALPHA * s
        r2 = u + BETA * l1
        l2 = l1 + GAMMA * (t + BETA * l1 + r2)
        out.append((l1, l2, s, r2))
    return out


def _boundaries(own_even, own_odd, got_even, got_odd, bnd, count):
    odd = lax.axis_index("row") % 2 == 1

    def read(ref):
        return [ref[pl.ds(k * TILES, count), :] for k in range(6)]

    oe, oo, ge, go = read(own_even), read(own_odd), read(got_even), read(got_odd)

    def pick(yes, no):
        return [jnp.where(odd, y, n) for y, n in zip(yes, no)]

    top = _junction(pick(ge, go), pick(oe, oo))
    low = _junction(pick(oo, oe), pick(go, ge))
    for level in range(3):
        for j in range(4):
            bnd[pl.ds((level * 4 + j) * count, count), :] = (top if j < 2 else low)[level][j]


def _rows_transform(tile, edge):
    row = lax.axis_index("row")
    sub = _sub()
    is7, is0 = sub == 7, sub == 0
    mir7 = is7 & (row == lax.axis_size("row") - 1)
    mir0 = is0 & (row == 0)
    odd = (sub & 1) == 1
    zero = jnp.zeros((8, LANES), F32)

    def up(v, level, j, mirror):
        return jnp.where(mir7, mirror, jnp.where(is7, edge(level, j), pltpu.roll(v, 7, 0)))

    def dn(v, level, j, mirror):
        return jnp.where(mir0, mirror, jnp.where(is0, edge(level, j), pltpu.roll(v, 1, 0)))

    a, b, c, d = tile
    c1 = c + ALPHA * (a + b)
    d1 = d + ALPHA * (b + up(a, 0, 2, b))
    a1 = a + BETA * (dn(d1, 0, 0, c1) + c1)
    b1 = b + BETA * (c1 + d1)
    c2 = c1 + GAMMA * (a1 + b1)
    d2 = d1 + GAMMA * (b1 + up(a1, 0, 3, b1))
    a = (a1 + DELTA * (dn(d2, 0, 1, c2) + c2)) * SCALE_LOW
    b = (b1 + DELTA * (c2 + d2)) * SCALE_LOW
    v = [a, b, c2 * SCALE_HIGH, d2 * SCALE_HIGH]
    b1 = b + ALPHA * (a + up(a, 1, 2, a))
    a1 = a + BETA * (dn(b1, 1, 0, b1) + b1)
    b2 = b1 + GAMMA * (a1 + up(a1, 1, 3, a1))
    x = (a1 + DELTA * (dn(b2, 1, 1, b2) + b2)) * SCALE_LOW
    v += [x, b2 * SCALE_HIGH]
    for ka, kb, j in ((ALPHA, BETA, 0), (GAMMA, DELTA, 1)):
        back = pltpu.roll(x, 1, 0)
        x = x + jnp.where(odd, ka, zero) * (back + up(x, 2, 2 + j, back))
        ahead = pltpu.roll(x, 7, 0)
        x = x + jnp.where(odd, zero, kb) * (dn(x, 2, j, ahead) + ahead)
    v.append(x * jnp.where(odd, SCALE_HIGH, zero + SCALE_LOW))
    return v


def states_kernel(x_ref, even_ref, odd_ref, scr, sems):
    copies = [
        [
            _load(
                x_ref.at[img, rt],
                scr.at[pl.ds(img * CHUNKS, CHUNKS), pl.ds(rt * 8, 8), :],
                sems.at[img, rt],
            )
            for rt in range(4)
        ]
        for img in range(IMAGES)
    ]
    is_odd = lax.axis_index("row") % 2 == 1
    for img in range(IMAGES):
        for copy in copies[img]:
            copy.wait()
        for group in range(0, CHUNKS, 4):
            got = [
                (tile_row(img, c), *_states_of(_rows_of(scr, img * CHUNKS + c))) for c in range(group, group + 4)
            ]

            def put(to_end, to_start):
                for t, end, start in got:
                    for k in range(6):
                        to_end[pl.ds(k * TILES + t, 1), :] = end[k]
                        to_start[pl.ds(k * TILES + t, 1), :] = start[k]

            pl.when(is_odd)(lambda: put(odd_ref, even_ref))
            pl.when(jnp.logical_not(is_odd))(lambda: put(even_ref, odd_ref))


def edges_kernel(x_ref, own_even, own_odd, got_even, got_odd, v_ref, even_ref, odd_ref, scr, bnd, sems):
    copies = []
    for side, chunk in enumerate((0, CHUNKS - 1)):
        for img in range(IMAGES):
            for rt in range(4):
                copies.append(
                    _load(
                        x_ref.at[img, rt, chunk],
                        scr.at[side * IMAGES + img, pl.ds(rt * 8, 8), :],
                        sems.at[side * IMAGES + img, rt],
                    )
                )
    _boundaries(own_even, own_odd, got_even, got_odd, bnd, EDGES)
    for copy in copies:
        copy.wait()
    lane = _lane()
    zero = jnp.zeros((8, LANES), F32)
    tiles = []
    for t in range(EDGES):

        def edge(level, j, t=t):
            return jnp.broadcast_to(bnd[pl.ds((level * 4 + j) * EDGES + t, 1), :], (8, LANES))

        v = _rows_transform(_rows_of(scr, t), edge)
        for k in range(7):
            v_ref[t, k] = v[k]
        tiles.append(v)
    is_odd = lax.axis_index("col") % 2 == 1
    for n, (base, count, width) in enumerate(KINDS):
        to_left, to_right = zero, zero
        for img in range(IMAGES):
            for q in range(count):
                slot = (img * count + q) * width
                here = (lane >= slot) & (lane < slot + width)
                start, end = tiles[img][base + q], tiles[IMAGES + img][base + q]
                if slot:
                    start = pltpu.roll(start, slot, 1)
                if (slot + width) % LANES:
                    end = pltpu.roll(end, slot + width, 1)
                to_left = jnp.where(here, start, to_left)
                to_right = jnp.where(here, end, to_right)
        even_ref[pl.ds(8 * n, 8), :] = jnp.where(is_odd, to_left, to_right)
        odd_ref[pl.ds(8 * n, 8), :] = jnp.where(is_odd, to_right, to_left)


def main_kernel(x_ref, own_even, own_odd, got_even, got_odd, out_ref, edge_ref, scr, vs, bnd, in_sems, out_sems):
    copies = [
        [
            _load(
                x_ref.at[img, rt],
                scr.at[pl.ds(img * CHUNKS, CHUNKS), pl.ds(rt * 8, 8), :],
                in_sems.at[img, rt],
            )
            for rt in range(4)
        ]
        for img in range(IMAGES)
    ]
    _boundaries(own_even, own_odd, got_even, got_odd, bnd, TILES)
    lane = _lane()

    def band_pass(xs, level):
        st = 1 << level
        pos = lane & (2 * st - 1)
        is_low, is_high = pos == 0, pos == st
        rolls = [
            {k: pltpu.roll(x, (k * st) % LANES, 1) for k in (-4, -3, -2, -1, 1, 2, 3, 4)} for x in xs
        ]
        coefs = [jnp.where(is_low, LOW[4 + k], jnp.where(is_high, HIGH[4 + k], 0.0)).astype(F32) for k in range(5)]
        out = []
        for c in range(CHUNKS):
            acc = coefs[0] * xs[c]
            for k in range(1, 5):
                before, after = rolls[c][k], rolls[c][-k]
                if c:
                    before = jnp.where(lane < k * st, rolls[c - 1][k], before)
                if c < CHUNKS - 1:
                    after = jnp.where(lane >= LANES - k * st, rolls[c + 1][-k], after)
                acc = acc + coefs[k] * (before + after)
            out.append(acc)
        return out

    def line(k):
        return [vs[k, c] for c in range(CHUNKS)]

    def image(img):
        for c in range(CHUNKS):

            def edge(level, j, c=c):
                t = tile_row(img, c)
                return jnp.broadcast_to(bnd[pl.ds((level * 4 + j) * TILES + t, 1), :], (8, LANES))

            v = _rows_transform(_rows_of(scr, img * CHUNKS + c), edge)
            for k in range(7):
                vs[k, c] = v[k]

        def put(k, keep, xs):
            for c in range(CHUNKS):
                where = (img * CHUNKS + c, pl.ds(OFFSETS[k], 8, stride=4), slice(None))
                scr[where] = xs[c] if keep is None else jnp.where(keep, xs[c], scr[where])

        for k in range(4):
            put(k, None, band_pass(line(k), 0))
        for k in range(2):
            put(k, (lane & 1) == 0, band_pass(band_pass(line(4 + k), 0), 1))
        put(0, (lane & 3) == 0, band_pass(band_pass(band_pass(line(6), 0), 1), 2))
        for side, chunk in enumerate((0, CHUNKS - 1)):
            edge_ref[side * IMAGES + img] = scr[img * CHUNKS + chunk]

    stores = []
    for img in range(IMAGES):
        for copy in copies[img]:
            copy.wait()
        image(img)
        for rt in range(4):
            stores.append(
                _load(
                    scr.at[pl.ds(img * CHUNKS + 1, CHUNKS - 2), pl.ds(rt * 8, 8), :],
                    out_ref.at[img, rt, pl.ds(1, CHUNKS - 2)],
                    out_sems.at[img, rt],
                )
            )
    for copy in stores:
        copy.wait()


def patch_kernel(taps_ref, v_ref, edge_in, got_even, got_odd, dest_ref, out_ref, scr, sems):
    del dest_ref
    col = lax.axis_index("col")
    is_odd = col % 2 == 1
    at_edge = (jnp.where(col == 0, 1, 0), jnp.where(col == lax.axis_size("col") - 1, 1, 0))
    lane = _lane()
    low_half = lane < HALF
    windows = ([], [])
    for n, (base, count, width) in enumerate(KINDS):
        via_even, via_odd = got_even[pl.ds(8 * n, 8), :], got_odd[pl.ds(8 * n, 8), :]
        got = (jnp.where(is_odd, via_even, via_odd), jnp.where(is_odd, via_odd, via_even))
        for img in range(IMAGES):
            for q in range(count):
                slot = (img * count + q) * width
                for side, shift in ((0, HALF - slot - width), (1, HALF - slot)):
                    halo = pltpu.roll(got[side], shift % LANES, 1) if shift % LANES else got[side]
                    own = pltpu.roll(v_ref[side * IMAGES + img, base + q], HALF, 1)
                    first, second = (halo, own) if side == 0 else (own, halo)
                    windows[side].append((img, base + q, jnp.where(low_half, first, second)))

    def band_pass(xs, side, level):
        row = side * 2 + at_edge[side]
        coefs = [
            jnp.broadcast_to(taps_ref[row, pl.ds(level * 9 + k, 1), :], (8, LANES)) for k in range(9)
        ]
        st = 1 << level
        out = []
        for x in xs:
            acc = coefs[4] * x
            for k in (-4, -3, -2, -1, 1, 2, 3, 4):
                acc = acc + coefs[4 + k] * pltpu.roll(x, (-k * st) % LANES, 1)
            out.append(acc)
        return out

    copies = []
    for side in range(2):
        keys = [(img, k) for img, k, _ in windows[side]]
        xs = band_pass([w for _, _, w in windows[side]], side, 0)
        done = dict(zip(keys, xs))
        deeper = [key for key in keys if key[1] >= 4]
        done.update(zip(deeper, band_pass([done[key] for key in deeper], side, 1)))
        deepest = [key for key in keys if key[1] >= 6]
        done.update(zip(deepest, band_pass([done[key] for key in deepest], side, 2)))
        inside = lane < PATCH if side == 0 else lane >= LANES - PATCH
        for img in range(IMAGES):
            t = side * IMAGES + img
            for q in range(4):
                new = done[img, q]
                if q < 2:
                    new = jnp.where((lane & 1) == 0, done[img, 4 + q], new)
                if q < 1:
                    new = jnp.where((lane & 3) == 0, done[img, 6], new)
                where = (t, pl.ds(OFFSETS[q], 8, stride=4), slice(None))
                scr[where] = jnp.where(inside, pltpu.roll(new, HALF, 1), edge_in[where])
            for rt in range(4):
                copies.append(
                    _load(
                        scr.at[t, pl.ds(rt * 8, 8), :],
                        out_ref.at[img, rt, (CHUNKS - 1) * side],
                        sems.at[t, rt],
                    )
                )
    for copy in copies:
        copy.wait()


def swap(axis, even, odd):
    n = lax.axis_size(axis)
    even_pairs = [(i, i ^ 1) for i in range(n)]
    odd_pairs = [(i, (i + 1 if i % 2 else i - 1) % n) for i in range(n)]
    return lax.ppermute(even, axis, even_pairs), lax.ppermute(odd, axis, odd_pairs)


VMEM = pl.BlockSpec(memory_space=pltpu.VMEM)
ANY = pl.BlockSpec(memory_space=pl.ANY)


def shape(*dims):
    return jax.ShapeDtypeStruct(dims, F32)


def shards(images):
    x = images.reshape(IMAGES, 4, 8, CHUNKS, LANES).transpose(0, 1, 3, 2, 4)
    dma = pltpu.SemaphoreType.DMA
    row_even, row_odd = pl.pallas_call(
        states_kernel,
        out_shape=(shape(6 * TILES, LANES), shape(6 * TILES, LANES)),
        in_specs=[ANY],
        out_specs=(VMEM, VMEM),
        scratch_shapes=[pltpu.VMEM((TILES, ROWS, LANES), F32), dma((IMAGES, 4))],
        name="row_states",
    )(x)
    got_even, got_odd = swap("row", row_even, row_odd)
    rows = (row_even, row_odd, got_even, got_odd)
    v_edge, col_even, col_odd = pl.pallas_call(
        edges_kernel,
        out_shape=(shape(EDGES, 7, 8, LANES), shape(24, LANES), shape(24, LANES)),
        in_specs=[ANY] + [VMEM] * 4,
        out_specs=(VMEM,) * 3,
        scratch_shapes=[
            pltpu.VMEM((EDGES, ROWS, LANES), F32),
            pltpu.VMEM((12 * EDGES, LANES), F32),
            dma((EDGES, 4)),
        ],
        name="edge_rows",
    )(x, *rows)
    halo_even, halo_odd = swap("col", col_even, col_odd)
    out, out_edge = pl.pallas_call(
        main_kernel,
        out_shape=(shape(IMAGES, 4, CHUNKS, 8, LANES), shape(EDGES, ROWS, LANES)),
        in_specs=[ANY] + [VMEM] * 4,
        out_specs=(ANY, VMEM),
        scratch_shapes=[
            pltpu.VMEM((TILES, ROWS, LANES), F32),
            pltpu.VMEM((7, CHUNKS, 8, LANES), F32),
            pltpu.VMEM((12 * TILES, LANES), F32),
            dma((IMAGES, 4)),
            dma((IMAGES, 4)),
        ],
        cost_estimate=pl.CostEstimate(flops=40_000_000, transcendentals=0, bytes_accessed=2_000_000),
        name="interior",
    )(x, *rows)
    out = pl.pallas_call(
        patch_kernel,
        out_shape=shape(IMAGES, 4, CHUNKS, 8, LANES),
        in_specs=[VMEM] * 5 + [ANY],
        out_specs=ANY,
        input_output_aliases={5: 0},
        scratch_shapes=[pltpu.VMEM((EDGES, ROWS, LANES), F32), dma((EDGES, 4))],
        name="edge_columns",
    )(jnp.asarray(EDGE_TAPS), v_edge, out_edge, halo_even, halo_odd, out)
    return out.transpose(0, 1, 3, 2, 4).reshape(IMAGES, ROWS, CHUNKS * LANES)


def solution(mesh):
    return jax.shard_map(
        shards,
        mesh=mesh,
        in_specs=(P(None, "row", "col"),),
        out_specs=P(None, "row", "col"),
        check_vma=False,
    )
```

time: 320 us -> 37 us (0.12)
  the two profiles are of different devices: /device:TPU:30 before, /device:TPU:1 now
where the time goes in v2:
time: 37 us; the launch traced here: 36.6 us
  Pallas kernels  19.3 us (52%)
  starting transfers between devices  10.4 us (28%)
  waiting for transfers between devices  5.6 us (15%)
  local copies, waits for them, and re-layouts  1.28 us (3%)
    pallas_call x1, Pallas kernels, shards(): pl.pallas_call(main_kernel, out_shape=(shape(IMAGES, 4, CHUNKS, 8, LANES)...  10.1 us
    ppermute x2, starting transfers between devices, swap(): lax.ppermute(odd, axis, odd_pairs)  6.78 us
    ppermute x2, waiting for transfers between devices, swap(): lax.ppermute(odd, axis, odd_pairs)  4.32 us
    ppermute x2, starting transfers between devices, swap(): lax.ppermute(even, axis, even_pairs)  3.57 us
    pallas_call x1, Pallas kernels, shards(): pl.pallas_call(edges_kernel, out_shape=(shape(EDGES, 7, 8, LANES), shape(...  3.23 us
    pallas_call x1, Pallas kernels, shards(): pl.pallas_call(patch_kernel, out_shape=shape(IMAGES, 4, CHUNKS, 8, LANES)...  3.16 us
    pallas_call x1, Pallas kernels, shards(): pl.pallas_call(states_kernel, out_shape=(shape(6 * TILES, LANES), shape(6...  2.82 us
    ppermute x2, waiting for transfers between devices, swap(): lax.ppermute(even, axis, even_pairs)  1.28 us
  transfers between devices with their start and end apart: 4, of which 2 were waited for; matrix products, arithmetic and copies ran while one was open for 0% of the time, Pallas kernels for 28%

profile of v2, /device:TPU:1, one launch (start us, length us, event | category | flops | bytes accessed | tf_op | source)
XLA Modules:
  0.0 36.6 jit_solution(7617597853733870712)
XLA Ops:
  0.0 2.8 %row_states.1 = (f32[384,128]{1,0:T(8,128)}, f32[384,128]{1,0:T(8,128)}) custom-call(f32[4,4,16,8,128]{4,3,2,1,0:T(8,128)} %bitcast.6), custom_call_target="tpu_custom_call" | custom-call | tf_op jit(solution)/shard_map/row_states/pallas_call | solution.py:476
  2.8 3.5 %collective-permute-start = (f32[384,128]{1,0:T(8,128)}, f32[384,128]{1,0:T(8,128)S(1)}, u32[]{:S(2)}, u32[]{:S(2)}) collective-permute-start(f32[384,128]{1,0:T(8,128)} %get-tuple-element.12.own_even), channel_id=1, source_target_pairs={{0,32},{32,0},{64,96},{96,64},{128,160},{160,128},{192,224},{224,1... | collective-permute-start | bytes 589832 | tf_op jit(solution)/shard_map/ppermute | solution.py:462
  6.3 0.0 collective-permute-start.1
  6.3 1.3 %collective-permute-done.got_even = f32[384,128]{1,0:T(8,128)S(1)} collective-permute-done((f32[384,128]{1,0:T(8,128)}, f32[384,128]{1,0:T(8,128)S(1)}, u32[]{:S(2)}, u32[]{:S(2)}) %collective-permute-start) | collective-permute-done | bytes 196640 | tf_op jit(solution)/shard_map/ppermute | solution.py:462
  7.6 0.0 copy-start
  7.6 4.3 %collective-permute-done.1.got_odd = f32[384,128]{1,0:T(8,128)S(1)} collective-permute-done((f32[384,128]{1,0:T(8,128)}, f32[384,128]{1,0:T(8,128)S(1)}, u32[]{:S(2)}, u32[]{:S(2)}) %collective-permute-start.1) | collective-permute-done | bytes 196640 | tf_op jit(solution)/shard_map/ppermute | solution.py:462
  11.9 0.0 copy-done
  11.9 0.0 copy-start.1
  11.9 0.7 %copy-done.1 = f32[384,128]{1,0:T(8,128)} copy-done((f32[384,128]{1,0:T(8,128)}, f32[384,128]{1,0:T(8,128)S(1)}, u32[]{:S(2)}) %copy-start.1) | copy-done | bytes 196632
  12.6 3.2 %edge_rows.1 = (f32[8,7,8,128]{3,2,1,0:T(8,128)}, f32[24,128]{1,0:T(8,128)}, f32[24,128]{1,0:T(8,128)}) custom-call(f32[4,4,16,8,128]{4,3,2,1,0:T(8,128)} %bitcast.7, f32[384,128]{1,0:T(8,128)} %get-tuple-element.12.own_even, f32[384,128]{1,0:T(8,128)} %get-tuple-element.13.own_odd, f32[384,128]{1,0:T(8,128)} %copy-done, f32[384,128]{1,0:T(8,128)} %copy-done.1), custom_call_target="tpu_custom_call" | custom-call | tf_op jit(solution)/shard_map/edge_rows/pallas_call | solution.py:486
  15.8 0.1 collective-permute-start.2
  15.9 6.8 %collective-permute-start.3 = (f32[24,128]{1,0:T(8,128)}, f32[24,128]{1,0:T(8,128)S(1)}, u32[]{:S(2)}, u32[]{:S(2)}) collective-permute-start(f32[24,128]{1,0:T(8,128)} %get-tuple-element.17), channel_id=1, source_target_pairs={{0,31},{1,2},{2,1},{3,4},{4,3},{5,6},{6,5},{7,8},{8,7},{9,10},{10,... | collective-permute-start | bytes 36872 | tf_op jit(solution)/shard_map/ppermute | solution.py:462
  22.7 10.1 %interior.1 = (f32[4,4,16,8,128]{4,3,2,1,0:T(8,128)}, f32[8,32,128]{2,1,0:T(8,128)}) custom-call(f32[4,4,16,8,128]{4,3,2,1,0:T(8,128)} %bitcast.8, f32[384,128]{1,0:T(8,128)} %get-tuple-element.12.own_even, f32[384,128]{1,0:T(8,128)} %get-tuple-element.13.own_odd, f32[384,128]{1,0:T(8,128)} %copy-done, f32[384,128]{1,0:T(8,128)} %copy-done.1), custom_call_target="tpu_custom_call" | custom-call | flops 40000000 | bytes 2000000 | tf_op jit(solution)/shard_map/interior/pallas_call | solution.py:499
  32.8 0.0 collective-permute-done.2.got_even
  32.8 0.0 copy-start.2
  32.9 0.0 collective-permute-done.3.got_odd
  32.9 0.0 copy-start.3
  32.9 0.6 %copy-done.2 = f32[24,128]{1,0:T(8,128)} copy-done((f32[24,128]{1,0:T(8,128)}, f32[24,128]{1,0:T(8,128)S(1)}, u32[]{:S(2)}) %copy-start.2) | copy-done | bytes 12312
  33.4 0.0 copy-done.3
  33.5 3.2 %edge_columns.1 = f32[4,4,16,8,128]{4,3,2,1,0:T(8,128)} custom-call(f32[4,27,128]{2,1,0:T(8,128)} %constant.2.clone.taps_ref, f32[8,7,8,128]{3,2,1,0:T(8,128)} %get-tuple-element.14.v_ref, f32[8,32,128]{2,1,0:T(8,128)} %get-tuple-element.15.edge_in, f32[24,128]{1,0:T(8,128)} %copy-done.2, f32[24,128]{1,0:T(8,128)} %copy-done.3, ...), custom_call_target="tpu_custom_call", output_to_operand_aliasing={{}: (5, {})} | custom-call | tf_op jit(solution)/shard_map/edge_columns/pallas_call | solution.py:514
Async XLA Ops:
  2.8 4.8 %collective-permute-start = (f32[384,128]{1,0:T(8,128)}, f32[384,128]{1,0:T(8,128)S(1)}, u32[]{:S(2)}, u32[]{:S(2)}) collective-permute-start(f32[384,128]{1,0:T(8,128)} %get-tuple-element.12.own_even), channel_id=1, source_target_pairs={{0,32},{32,0},{64,96},{96,64},{128,160},{160,128},{192,224},{224,1... | collective-permute-start | bytes 589832 | tf_op jit(solution)/shard_map/ppermute | solution.py:462
  6.3 5.6 %collective-permute-start.1 = (f32[384,128]{1,0:T(8,128)}, f32[384,128]{1,0:T(8,128)S(1)}, u32[]{:S(2)}, u32[]{:S(2)}) collective-permute-start(f32[384,128]{1,0:T(8,128)} %get-tuple-element.13.own_odd), channel_id=1, source_target_pairs={{0,224},{32,64},{64,32},{96,128},{128,96},{160,192},{192,160},{224... | collective-permute-start | bytes 589832 | tf_op jit(solution)/shard_map/ppermute | solution.py:462
  7.6 4.3 %copy-start = (f32[384,128]{1,0:T(8,128)}, f32[384,128]{1,0:T(8,128)S(1)}, u32[]{:S(2)}) copy-start(f32[384,128]{1,0:T(8,128)S(1)} %collective-permute-done.got_even) | copy-start | bytes 589828
  11.9 0.7 %copy-start.1 = (f32[384,128]{1,0:T(8,128)}, f32[384,128]{1,0:T(8,128)S(1)}, u32[]{:S(2)}) copy-start(f32[384,128]{1,0:T(8,128)S(1)} %collective-permute-done.1.got_odd) | copy-start | bytes 589828
  15.8 17.0 %collective-permute-start.2 = (f32[24,128]{1,0:T(8,128)}, f32[24,128]{1,0:T(8,128)S(1)}, u32[]{:S(2)}, u32[]{:S(2)}) collective-permute-start(f32[24,128]{1,0:T(8,128)} %get-tuple-element.16), channel_id=1, source_target_pairs={{0,1},{1,0},{2,3},{3,2},{4,5},{5,4},{6,7},{7,6},{8,9},{9,8},{10,11... | collective-permute-start | bytes 36872 | tf_op jit(solution)/shard_map/ppermute | solution.py:462
  15.9 16.9 %collective-permute-start.3 = (f32[24,128]{1,0:T(8,128)}, f32[24,128]{1,0:T(8,128)S(1)}, u32[]{:S(2)}, u32[]{:S(2)}) collective-permute-start(f32[24,128]{1,0:T(8,128)} %get-tuple-element.17), channel_id=1, source_target_pairs={{0,31},{1,2},{2,1},{3,4},{4,3},{5,6},{6,5},{7,8},{8,7},{9,10},{10,... | collective-permute-start | bytes 36872 | tf_op jit(solution)/shard_map/ppermute | solution.py:462
  32.8 0.6 %copy-start.2 = (f32[24,128]{1,0:T(8,128)}, f32[24,128]{1,0:T(8,128)S(1)}, u32[]{:S(2)}) copy-start(f32[24,128]{1,0:T(8,128)S(1)} %collective-permute-done.2.got_even) | copy-start | bytes 36868
  32.9 0.6 %copy-start.3 = (f32[24,128]{1,0:T(8,128)}, f32[24,128]{1,0:T(8,128)S(1)}, u32[]{:S(2)}) copy-start(f32[24,128]{1,0:T(8,128)S(1)} %collective-permute-done.3.got_odd) | copy-start | bytes 36868

commit v3 on v2

--- a/solution.py
+++ b/solution.py
@@ -5,6 +5,7 @@
 from jax.experimental import pallas as pl
 from jax.experimental.pallas import tpu as pltpu
 from jax.sharding import PartitionSpec as P
+
 
 ALPHA = -1.586134342
 BETA = -0.05298011854
@@ -264,21 +265,8 @@
             pl.when(jnp.logical_not(is_odd))(lambda: put(even_ref, odd_ref))
 
 
-def edges_kernel(x_ref, own_even, own_odd, got_even, got_odd, v_ref, even_ref, odd_ref, scr, bnd, sems):
-    copies = []
-    for side, chunk in enumerate((0, CHUNKS - 1)):
-        for img in range(IMAGES):
-            for rt in range(4):
-                copies.append(
-                    _load(
-                        x_ref.at[img, rt, chunk],
-                        scr.at[side * IMAGES + img, pl.ds(rt * 8, 8), :],
-                        sems.at[side * IMAGES + img, rt],
-                    )
-                )
+def edges_kernel(x_ref, own_even, own_odd, got_even, got_odd, v_ref, even_ref, odd_ref, bnd):
     _boundaries(own_even, own_odd, got_even, got_odd, bnd, EDGES)
-    for copy in copies:
-        copy.wait()
     lane = _lane()
     zero = jnp.zeros((8, LANES), F32)
     tiles = []
@@ -287,7 +275,8 @@
         def edge(level, j, t=t):
             return jnp.broadcast_to(bnd[pl.ds((level * 4 + j) * EDGES + t, 1), :], (8, LANES))
 
-        v = _rows_transform(_rows_of(scr, t), edge)
+        column = (t % IMAGES) * CHUNKS + (t // IMAGES) * (CHUNKS - 1)
+        v = _rows_transform(_rows_of(x_ref, column), edge)
         for k in range(7):
             v_ref[t, k] = v[k]
         tiles.append(v)
@@ -309,18 +298,7 @@
         odd_ref[pl.ds(8 * n, 8), :] = jnp.where(is_odd, to_right, to_left)
 
 
-def main_kernel(x_ref, own_even, own_odd, got_even, got_odd, out_ref, edge_ref, scr, vs, bnd, in_sems, out_sems):
-    copies = [
-        [
-            _load(
-                x_ref.at[img, rt],
-                scr.at[pl.ds(img * CHUNKS, CHUNKS), pl.ds(rt * 8, 8), :],
-                in_sems.at[img, rt],
-            )
-            for rt in range(4)
-        ]
-        for img in range(IMAGES)
-    ]
+def main_kernel(x_ref, own_even, own_odd, got_even, got_odd, out_ref, edge_ref, scr, vs, bnd, sems):
     _boundaries(own_even, own_odd, got_even, got_odd, bnd, TILES)
     lane = _lane()
 
@@ -355,7 +333,7 @@
                 t = tile_row(img, c)
                 return jnp.broadcast_to(bnd[pl.ds((level * 4 + j) * TILES + t, 1), :], (8, LANES))
 
-            v = _rows_transform(_rows_of(scr, img * CHUNKS + c), edge)
+            v = _rows_transform(_rows_of(x_ref, img * CHUNKS + c), edge)
             for k in range(7):
                 vs[k, c] = v[k]
 
@@ -374,15 +352,13 @@
 
     stores = []
     for img in range(IMAGES):
-        for copy in copies[img]:
-            copy.wait()
         image(img)
         for rt in range(4):
             stores.append(
                 _load(
                     scr.at[pl.ds(img * CHUNKS + 1, CHUNKS - 2), pl.ds(rt * 8, 8), :],
                     out_ref.at[img, rt, pl.ds(1, CHUNKS - 2)],
-                    out_sems.at[img, rt],
+                    sems.at[img, rt],
                 )
             )
     for copy in stores:
@@ -458,8 +434,18 @@
 def swap(axis, even, odd):
     n = lax.axis_size(axis)
     even_pairs = [(i, i ^ 1) for i in range(n)]
-    odd_pairs = [(i, (i + 1 if i % 2 else i - 1) % n) for i in range(n)]
-    return lax.ppermute(even, axis, even_pairs), lax.ppermute(odd, axis, odd_pairs)
+    odd_pairs = [(i, i + 1 if i % 2 else i - 1) for i in range(1, n - 1)] + [(0, 0), (n - 1, n - 1)]
+    via_odd = lax.ppermute(odd, axis, odd_pairs)
+    via_even = lax.ppermute(even, axis, even_pairs)
+    return near(via_even), near(via_odd)
+
+
+def near(value):
+    return pltpu.with_memory_space_constraint(value, pltpu.VMEM)
+
+
+def held(*dims):
+    return pltpu.VMEM(dims, F32)
 
 
 VMEM = pl.BlockSpec(memory_space=pltpu.VMEM)
@@ -470,47 +456,42 @@
     return jax.ShapeDtypeStruct(dims, F32)
 
 
-def shards(images):
+def transform(images):
     x = images.reshape(IMAGES, 4, 8, CHUNKS, LANES).transpose(0, 1, 3, 2, 4)
     dma = pltpu.SemaphoreType.DMA
-    row_even, row_odd = pl.pallas_call(
+    row_even, row_odd, block = pl.pallas_call(
         states_kernel,
-        out_shape=(shape(6 * TILES, LANES), shape(6 * TILES, LANES)),
+        out_shape=(held(6 * TILES, LANES), held(6 * TILES, LANES), held(TILES, ROWS, LANES)),
         in_specs=[ANY],
-        out_specs=(VMEM, VMEM),
-        scratch_shapes=[pltpu.VMEM((TILES, ROWS, LANES), F32), dma((IMAGES, 4))],
+        out_specs=(VMEM,) * 3,
+        scratch_shapes=[dma((IMAGES, 4))],
         name="row_states",
     )(x)
     got_even, got_odd = swap("row", row_even, row_odd)
-    rows = (row_even, row_odd, got_even, got_odd)
+    rows = (near(block), near(row_even), near(row_odd), got_even, got_odd)
     v_edge, col_even, col_odd = pl.pallas_call(
         edges_kernel,
-        out_shape=(shape(EDGES, 7, 8, LANES), shape(24, LANES), shape(24, LANES)),
-        in_specs=[ANY] + [VMEM] * 4,
+        out_shape=(held(EDGES, 7, 8, LANES), held(24, LANES), held(24, LANES)),
+        in_specs=[VMEM] * 5,
         out_specs=(VMEM,) * 3,
-        scratch_shapes=[
-            pltpu.VMEM((EDGES, ROWS, LANES), F32),
-            pltpu.VMEM((12 * EDGES, LANES), F32),
-            dma((EDGES, 4)),
-        ],
+        scratch_shapes=[pltpu.VMEM((12 * EDGES, LANES), F32)],
         name="edge_rows",
-    )(x, *rows)
+    )(*rows)
     halo_even, halo_odd = swap("col", col_even, col_odd)
     out, out_edge = pl.pallas_call(
         main_kernel,
-        out_shape=(shape(IMAGES, 4, CHUNKS, 8, LANES), shape(EDGES, ROWS, LANES)),
-        in_specs=[ANY] + [VMEM] * 4,
+        out_shape=(shape(IMAGES, 4, CHUNKS, 8, LANES), held(EDGES, ROWS, LANES)),
+        in_specs=[VMEM] * 5,
         out_specs=(ANY, VMEM),
         scratch_shapes=[
             pltpu.VMEM((TILES, ROWS, LANES), F32),
             pltpu.VMEM((7, CHUNKS, 8, LANES), F32),
             pltpu.VMEM((12 * TILES, LANES), F32),
             dma((IMAGES, 4)),
-            dma((IMAGES, 4)),
         ],
         cost_estimate=pl.CostEstimate(flops=40_000_000, transcendentals=0, bytes_accessed=2_000_000),
         name="interior",
-    )(x, *rows)
+    )(*rows)
     out = pl.pallas_call(
         patch_kernel,
         out_shape=shape(IMAGES, 4, CHUNKS, 8, LANES),
@@ -519,13 +500,13 @@
         input_output_aliases={5: 0},
         scratch_shapes=[pltpu.VMEM((EDGES, ROWS, LANES), F32), dma((EDGES, 4))],
         name="edge_columns",
-    )(jnp.asarray(EDGE_TAPS), v_edge, out_edge, halo_even, halo_odd, out)
+    )(near(jnp.asarray(EDGE_TAPS)), near(v_edge), near(out_edge), halo_even, halo_odd, out)
     return out.transpose(0, 1, 3, 2, 4).reshape(IMAGES, ROWS, CHUNKS * LANES)
 
 
 def solution(mesh):
     return jax.shard_map(
-        shards,
+        transform,
         mesh=mesh,
         in_specs=(P(None, "row", "col"),),
         out_specs=P(None, "row", "col"),

time: 37 us -> 28.2 us (0.76)
  the two profiles are of different devices: /device:TPU:1 before, /device:TPU:7 now
where the time goes in v3:
time: 28.2 us; the launch traced here: 28 us
  starting transfers between devices  12.7 us (45%)
  Pallas kernels  11.4 us (40%)
  waiting for transfers between devices  3.86 us (14%)
    ppermute x2, starting transfers between devices, swap(): via_odd = lax.ppermute(odd, axis, odd_pairs)  10.1 us
    pallas_call x1, Pallas kernels, transform(): pl.pallas_call(main_kernel, out_shape=(shape(IMAGES, 4, CHUNKS, 8, LANES)...  6.97 us
    ppermute x2, waiting for transfers between devices, swap(): via_odd = lax.ppermute(odd, axis, odd_pairs)  3.86 us
    ppermute x2, starting transfers between devices, swap(): via_even = lax.ppermute(even, axis, even_pairs)  2.66 us
    pallas_call x1, Pallas kernels, transform(): pl.pallas_call(patch_kernel, out_shape=shape(IMAGES, 4, CHUNKS, 8, LANES)...  2.1 us
    pallas_call x1, Pallas kernels, transform(): pl.pallas_call(states_kernel, out_shape=(held(6 * TILES, LANES), held(6 *...  2.07 us
  transfers between devices with their start and end apart: 4, of which 1 were waited for; matrix products, arithmetic and copies ran while one was open for 0% of the time, Pallas kernels for 25%

profile of v3, /device:TPU:7, one launch (start us, length us, event | category | flops | bytes accessed | tf_op | source)
XLA Modules:
  0.0 28.0 jit_solution(17767375011671276261)
XLA Ops:
  0.0 2.1 %row_states.1 = (f32[384,128]{1,0:T(8,128)S(1)}, f32[384,128]{1,0:T(8,128)S(1)}, f32[64,32,128]{2,1,0:T(8,128)S(1)}) custom-call(f32[4,4,16,8,128]{4,3,2,1,0:T(8,128)} %bitcast.6), custom_call_target="tpu_custom_call" | custom-call | tf_op jit(solution)/shard_map/row_states/pallas_call | solution.py:462
  2.1 1.0 %collective-permute-start = (f32[384,128]{1,0:T(8,128)S(1)}, f32[384,128]{1,0:T(8,128)S(1)}, u32[]{:S(2)}, u32[]{:S(2)}) collective-permute-start(f32[384,128]{1,0:T(8,128)S(1)} %get-tuple-element.14.own_even), channel_id=1, source_target_pairs={{0,32},{32,0},{64,96},{96,64},{128,160},{160,128},{192,224},{224,1... | collective-permute-start | bytes 589832 | tf_op jit(solution)/shard_map/ppermute | solution.py:439
  3.0 3.1 %collective-permute-start.1 = (f32[384,128]{1,0:T(8,128)S(1)}, f32[384,128]{1,0:T(8,128)S(1)}, u32[]{:S(2)}, u32[]{:S(2)}) collective-permute-start(f32[384,128]{1,0:T(8,128)S(1)} %get-tuple-element.15.own_odd), channel_id=1, source_target_pairs={{32,64},{64,32},{96,128},{128,96},{160,192},{192,160},{0,0},{224,2... | collective-permute-start | bytes 589832 | tf_op jit(solution)/shard_map/ppermute | solution.py:438
  6.1 0.0 collective-permute-done.got_even
  6.2 3.9 %collective-permute-done.1.got_odd = f32[384,128]{1,0:T(8,128)S(1)} collective-permute-done((f32[384,128]{1,0:T(8,128)S(1)}, f32[384,128]{1,0:T(8,128)S(1)}, u32[]{:S(2)}, u32[]{:S(2)}) %collective-permute-start.1) | collective-permute-done | bytes 196640 | tf_op jit(solution)/shard_map/ppermute | solution.py:438
  10.0 0.2 edge_rows.1
  10.2 1.7 %collective-permute-start.2 = (f32[24,128]{1,0:T(8,128)S(1)}, f32[24,128]{1,0:T(8,128)S(1)}, u32[]{:S(2)}, u32[]{:S(2)}) collective-permute-start(f32[24,128]{1,0:T(8,128)S(1)} %get-tuple-element.18), channel_id=1, source_target_pairs={{0,1},{1,0},{2,3},{3,2},{4,5},{5,4},{6,7},{7,6},{8,9},{9,8},{10,11... | collective-permute-start | bytes 36872 | tf_op jit(solution)/shard_map/ppermute | solution.py:439
  11.9 0.0 copy-start
  11.9 7.0 %collective-permute-start.3 = (f32[24,128]{1,0:T(8,128)S(1)}, f32[24,128]{1,0:T(8,128)S(1)}, u32[]{:S(2)}, u32[]{:S(2)}) collective-permute-start(f32[24,128]{1,0:T(8,128)S(1)} %get-tuple-element.19), channel_id=1, source_target_pairs={{1,2},{2,1},{3,4},{4,3},{5,6},{6,5},{7,8},{8,7},{9,10},{10,9},{11,... | collective-permute-start | bytes 36872 | tf_op jit(solution)/shard_map/ppermute | solution.py:438
  18.9 7.0 %interior.1 = (f32[4,4,16,8,128]{4,3,2,1,0:T(8,128)}, f32[8,32,128]{2,1,0:T(8,128)S(1)}) custom-call(f32[64,32,128]{2,1,0:T(8,128)S(1)} %get-tuple-element.13.x_ref, f32[384,128]{1,0:T(8,128)S(1)} %get-tuple-element.14.own_even, f32[384,128]{1,0:T(8,128)S(1)} %get-tuple-element.15.own_odd, f32[384,128]{1,0:T(8,128)S(1)} %collective-permute-done.got_even, ...), custom_call_target="tpu_custom_call" | custom-call | flops 40000000 | bytes 2000000 | tf_op jit(solution)/shard_map/interior/pallas_call | solution.py:481
  25.9 0.0 collective-permute-done.2.got_even
  25.9 0.0 collective-permute-done.3.got_odd
  25.9 0.0 copy-done
  25.9 2.1 %edge_columns.1 = f32[4,4,16,8,128]{4,3,2,1,0:T(8,128)} custom-call(f32[4,27,128]{2,1,0:T(8,128)S(1)} %copy-done, f32[8,7,8,128]{3,2,1,0:T(8,128)S(1)} %get-tuple-element.16.v_ref, f32[8,32,128]{2,1,0:T(8,128)S(1)} %get-tuple-element.17.edge_in, f32[24,128]{1,0:T(8,128)S(1)} %collective-permute-done.2.got_even, ...), custom_call_target="tpu_custom_call", output_to_operand_aliasing={{}: (5, {})} | custom-call | tf_op jit(solution)/shard_map/edge_columns/pallas_call | solution.py:495
Async XLA Ops:
  2.1 4.1 %collective-permute-start = (f32[384,128]{1,0:T(8,128)S(1)}, f32[384,128]{1,0:T(8,128)S(1)}, u32[]{:S(2)}, u32[]{:S(2)}) collective-permute-start(f32[384,128]{1,0:T(8,128)S(1)} %get-tuple-element.14.own_even), channel_id=1, source_target_pairs={{0,32},{32,0},{64,96},{96,64},{128,160},{160,128},{192,224},{224,1... | collective-permute-start | bytes 589832 | tf_op jit(solution)/shard_map/ppermute | solution.py:439
  3.0 7.0 %collective-permute-start.1 = (f32[384,128]{1,0:T(8,128)S(1)}, f32[384,128]{1,0:T(8,128)S(1)}, u32[]{:S(2)}, u32[]{:S(2)}) collective-permute-start(f32[384,128]{1,0:T(8,128)S(1)} %get-tuple-element.15.own_odd), channel_id=1, source_target_pairs={{32,64},{64,32},{96,128},{128,96},{160,192},{192,160},{0,0},{224,2... | collective-permute-start | bytes 589832 | tf_op jit(solution)/shard_map/ppermute | solution.py:438
  10.2 15.7 %collective-permute-start.2 = (f32[24,128]{1,0:T(8,128)S(1)}, f32[24,128]{1,0:T(8,128)S(1)}, u32[]{:S(2)}, u32[]{:S(2)}) collective-permute-start(f32[24,128]{1,0:T(8,128)S(1)} %get-tuple-element.18), channel_id=1, source_target_pairs={{0,1},{1,0},{2,3},{3,2},{4,5},{5,4},{6,7},{7,6},{8,9},{9,8},{10,11... | collective-permute-start | bytes 36872 | tf_op jit(solution)/shard_map/ppermute | solution.py:439
  11.9 14.0 %copy-start = (f32[4,27,128]{2,1,0:T(8,128)S(1)}, f32[4,27,128]{2,1,0:T(8,128)}, u32[]{:S(2)}) copy-start(f32[4,27,128]{2,1,0:T(8,128)} %constant.2.clone.taps_ref) | copy-start | bytes 165892
  11.9 14.0 %collective-permute-start.3 = (f32[24,128]{1,0:T(8,128)S(1)}, f32[24,128]{1,0:T(8,128)S(1)}, u32[]{:S(2)}, u32[]{:S(2)}) collective-permute-start(f32[24,128]{1,0:T(8,128)S(1)} %get-tuple-element.19), channel_id=1, source_target_pairs={{1,2},{2,1},{3,4},{4,3},{5,6},{6,5},{7,8},{8,7},{9,10},{10,9},{11,... | collective-permute-start | bytes 36872 | tf_op jit(solution)/shard_map/ppermute | solution.py:438

commit v4 on v3

--- a/solution.py
+++ b/solution.py
@@ -65,42 +65,69 @@
     return end, start
 
 
-def _taps():
-    low, high = [0.0] * 9, [0.0] * 9
-    for k in range(-4, 5):
-        x = [0.0] * 64
-        x[32 + k] = 1.0
-        low[k + 4] = _lift(x, (0.0, 0.0), (0.0, 0.0))[0][16]
-        x = [0.0] * 64
-        x[33 + k] = 1.0
-        high[k + 4] = _lift(x, (0.0, 0.0), (0.0, 0.0))[1][16]
-    return low, high
-
-
 END, START = _responses()
-LOW, HIGH = _taps()
-
-
-def _edge_taps():
-    table = np.zeros((2, 2, 3, 9, LANES), np.float32)
-    for side in range(2):
-        for mirrored in range(2):
-            for level in range(3):
-                st = 1 << level
-                for lane in range(0, LANES, st):
-                    taps = HIGH if (lane // st) % 2 else LOW
-                    for k in range(-4, 5):
-                        target = lane + k * st
-                        if mirrored and side == 0 and target < HALF <= lane:
-                            target = 2 * HALF - target
-                        edge = HALF - st
-                        if mirrored and side == 1 and target > edge >= lane:
-                            target = 2 * edge - target
-                        table[side, mirrored, level, (target - lane) // st + 4, lane] += taps[k + 4]
-    return table.reshape(2 * 2, 27, LANES)
-
-
-EDGE_TAPS = _edge_taps()
+
+
+def _levels(x, mirror):
+    out, st = [], 1
+    for _ in range(3):
+        s, d = list(x[0::2]), list(x[1::2])
+        m = len(s)
+        for odd, even in ((ALPHA, BETA), (GAMMA, DELTA)):
+            for i in range(m):
+                after = s[i + 1] if i + 1 < m else 0.0
+                if mirror and mirror[0] == 1 and (2 * i + 2) * st > mirror[1]:
+                    after = s[i]
+                d[i] = d[i] + odd * (s[i] + after)
+            for i in range(m):
+                before = d[i - 1] if i else 0.0
+                if mirror and mirror[0] == 0 and 2 * i * st == mirror[1]:
+                    before = d[i]
+                s[i] = s[i] + even * (before + d[i])
+        s, d = [v * SCALE_LOW for v in s], [v * SCALE_HIGH for v in d]
+        now = {2 * i * st: v for i, v in enumerate(s)}
+        now.update({(2 * i + 1) * st: v for i, v in enumerate(d)})
+        out.append(now)
+        x, st = s, 2 * st
+    return out
+
+
+def _matrices(span, taken, given, mirror=None):
+    table = np.zeros((3, taken[1], given[1]))
+    for k in range(taken[1]):
+        at = taken[0] + k
+        if mirror and (at < mirror[1] if mirror[0] == 0 else at > mirror[1]):
+            continue
+        x = [0.0] * span
+        x[at] = 1.0
+        for level, values in enumerate(_levels(x, mirror)):
+            for n in range(given[1]):
+                table[level, k, n] = values.get(given[0] + n, 0.0)
+    return table.astype(np.float32)
+
+
+def _parts(table):
+    high = table.astype(jnp.bfloat16)
+    return high, (table - high.astype(np.float32)).astype(jnp.bfloat16)
+
+
+def _line_matrices():
+    high, low = _parts(_matrices(4 * LANES, (LANES, 2 * LANES), (LANES + HALF, LANES)))
+    return np.concatenate([high, low], axis=2)
+
+
+def _edge_matrices():
+    out = []
+    for mirror in (None, (0, 2 * LANES), (1, 2 * LANES - 1)):
+        high, low = _parts(_matrices(4 * LANES, (2 * LANES - HALF, LANES), (2 * LANES - HALF, LANES), mirror))
+        top = np.concatenate([high, low], axis=2)
+        bottom = np.concatenate([high, np.zeros_like(high)], axis=2)
+        out.append(np.concatenate([top, bottom], axis=1))
+    return np.stack(out)
+
+
+LINE = _line_matrices()
+EDGE = _edge_matrices()
 
 
 def _sub():
@@ -298,81 +325,95 @@
         odd_ref[pl.ds(8 * n, 8), :] = jnp.where(is_odd, to_right, to_left)
 
 
-def main_kernel(x_ref, own_even, own_odd, got_even, got_odd, out_ref, edge_ref, scr, vs, bnd, sems):
+def _split(x):
+    high = x.astype(jnp.bfloat16)
+    return high, (x - high.astype(F32)).astype(jnp.bfloat16)
+
+
+def _dot(x, w):
+    return jnp.dot(x, w, preferred_element_type=F32)
+
+
+def main_kernel(w_ref, x_ref, own_even, own_odd, got_even, got_odd, out_ref, edge_ref, scr, lh1, ll1, lh2, ll2, lh3, ll3, bnd, sems):
     _boundaries(own_even, own_odd, got_even, got_odd, bnd, TILES)
     lane = _lane()
-
-    def band_pass(xs, level):
-        st = 1 << level
-        pos = lane & (2 * st - 1)
-        is_low, is_high = pos == 0, pos == st
-        rolls = [
-            {k: pltpu.roll(x, (k * st) % LANES, 1) for k in (-4, -3, -2, -1, 1, 2, 3, 4)} for x in xs
-        ]
-        coefs = [jnp.where(is_low, LOW[4 + k], jnp.where(is_high, HIGH[4 + k], 0.0)).astype(F32) for k in range(5)]
-        out = []
+    low_half = lane < HALF
+    lhs = ((lh1, ll1), (lh2, ll2), (lh3, ll3))
+
+    def build(pair):
+        before = None
+        for c in range(CHUNKS + 1):
+            now = before
+            if c < CHUNKS:
+                now = []
+                for img in pair:
+
+                    def edge(level, j, t=tile_row(img, c)):
+                        return jnp.broadcast_to(bnd[pl.ds((level * 4 + j) * TILES + t, 1), :], (8, LANES))
+
+                    v = _rows_transform(_rows_of(x_ref, img * CHUNKS + c), edge)
+                    now.append([pltpu.roll(tile, HALF, 1) for tile in v])
+            if before is None:
+                before = now
+            halves = [[jnp.where(low_half, p, q) for p, q in zip(ps, qs)] for ps, qs in zip(before, now)]
+            rows1 = [tile for half in halves for tile in half[:4]]
+            rows2 = [tile for half in halves for tile in half[4:6]]
+            rows3 = [half[6] for half in halves]
+            for (high_ref, low_ref), rows in zip(lhs, (rows1, rows2, rows3)):
+                high, low = _split(jnp.concatenate(rows, axis=0))
+                n = 8 * len(rows)
+                for ref, part in ((high_ref, high), (low_ref, low)):
+                    if c < CHUNKS:
+                        ref[pl.ds(c * n, n), pl.ds(0, LANES)] = part
+                    if c:
+                        ref[pl.ds((c - 1) * n, n), pl.ds(LANES, LANES)] = part
+            before = now
+
+    def multiply(pair):
+        outs = []
+        for kind, (high_ref, low_ref) in enumerate(lhs):
+            both = _dot(high_ref[...], w_ref[kind])
+            outs.append(both[:, :LANES] + both[:, LANES:] + _dot(low_ref[...], w_ref[kind, :, :LANES]))
         for c in range(CHUNKS):
-            acc = coefs[0] * xs[c]
-            for k in range(1, 5):
-                before, after = rolls[c][k], rolls[c][-k]
-                if c:
-                    before = jnp.where(lane < k * st, rolls[c - 1][k], before)
-                if c < CHUNKS - 1:
-                    after = jnp.where(lane >= LANES - k * st, rolls[c + 1][-k], after)
-                acc = acc + coefs[k] * (before + after)
-            out.append(acc)
-        return out
-
-    def line(k):
-        return [vs[k, c] for c in range(CHUNKS)]
-
-    def image(img):
-        for c in range(CHUNKS):
-
-            def edge(level, j, c=c):
-                t = tile_row(img, c)
-                return jnp.broadcast_to(bnd[pl.ds((level * 4 + j) * TILES + t, 1), :], (8, LANES))
-
-            v = _rows_transform(_rows_of(x_ref, img * CHUNKS + c), edge)
-            for k in range(7):
-                vs[k, c] = v[k]
-
-        def put(k, keep, xs):
-            for c in range(CHUNKS):
-                where = (img * CHUNKS + c, pl.ds(OFFSETS[k], 8, stride=4), slice(None))
-                scr[where] = xs[c] if keep is None else jnp.where(keep, xs[c], scr[where])
-
-        for k in range(4):
-            put(k, None, band_pass(line(k), 0))
-        for k in range(2):
-            put(k, (lane & 1) == 0, band_pass(band_pass(line(4 + k), 0), 1))
-        put(0, (lane & 3) == 0, band_pass(band_pass(band_pass(line(6), 0), 1), 2))
-        for side, chunk in enumerate((0, CHUNKS - 1)):
-            edge_ref[side * IMAGES + img] = scr[img * CHUNKS + chunk]
+            for i, img in enumerate(pair):
+                for q in range(4):
+                    at = (c * 2 + i) * 32 + q * 8
+                    val = outs[0][at : at + 8]
+                    if q < 2:
+                        at = (c * 2 + i) * 16 + q * 8
+                        val = jnp.where((lane & 1) == 0, outs[1][at : at + 8], val)
+                    if q < 1:
+                        at = (c * 2 + i) * 8
+                        val = jnp.where((lane & 3) == 0, outs[2][at : at + 8], val)
+                    scr[img * CHUNKS + c, pl.ds(OFFSETS[q], 8, stride=4), :] = val
 
     stores = []
-    for img in range(IMAGES):
-        image(img)
-        for rt in range(4):
-            stores.append(
-                _load(
-                    scr.at[pl.ds(img * CHUNKS + 1, CHUNKS - 2), pl.ds(rt * 8, 8), :],
-                    out_ref.at[img, rt, pl.ds(1, CHUNKS - 2)],
-                    sems.at[img, rt],
+    for pair in ((0, 1), (2, 3)):
+        build(pair)
+        multiply(pair)
+        for img in pair:
+            for side, chunk in enumerate((0, CHUNKS - 1)):
+                edge_ref[side * IMAGES + img] = scr[img * CHUNKS + chunk]
+            for rt in range(4):
+                stores.append(
+                    _load(
+                        scr.at[pl.ds(img * CHUNKS + 1, CHUNKS - 2), pl.ds(rt * 8, 8), :],
+                        out_ref.at[img, rt, pl.ds(1, CHUNKS - 2)],
+                        sems.at[img, rt],
+                    )
                 )
-            )
     for copy in stores:
         copy.wait()
 
 
-def patch_kernel(taps_ref, v_ref, edge_in, got_even, got_odd, dest_ref, out_ref, scr, sems):
+def patch_kernel(w_ref, v_ref, edge_in, got_even, got_odd, dest_ref, out_ref, scr, sems):
     del dest_ref
     col = lax.axis_index("col")
     is_odd = col % 2 == 1
-    at_edge = (jnp.where(col == 0, 1, 0), jnp.where(col == lax.axis_size("col") - 1, 1, 0))
+    which = (jnp.where(col == 0, 1, 0), jnp.where(col == lax.axis_size("col") - 1, 2, 0))
     lane = _lane()
     low_half = lane < HALF
-    windows = ([], [])
+    windows = [[[], [], []], [[], [], []]]
     for n, (base, count, width) in enumerate(KINDS):
         via_even, via_odd = got_even[pl.ds(8 * n, 8), :], got_odd[pl.ds(8 * n, 8), :]
         got = (jnp.where(is_odd, via_even, via_odd), jnp.where(is_odd, via_odd, via_even))
@@ -383,40 +424,25 @@
                     halo = pltpu.roll(got[side], shift % LANES, 1) if shift % LANES else got[side]
                     own = pltpu.roll(v_ref[side * IMAGES + img, base + q], HALF, 1)
                     first, second = (halo, own) if side == 0 else (own, halo)
-                    windows[side].append((img, base + q, jnp.where(low_half, first, second)))
-
-    def band_pass(xs, side, level):
-        row = side * 2 + at_edge[side]
-        coefs = [
-            jnp.broadcast_to(taps_ref[row, pl.ds(level * 9 + k, 1), :], (8, LANES)) for k in range(9)
-        ]
-        st = 1 << level
-        out = []
-        for x in xs:
-            acc = coefs[4] * x
-            for k in (-4, -3, -2, -1, 1, 2, 3, 4):
-                acc = acc + coefs[4 + k] * pltpu.roll(x, (-k * st) % LANES, 1)
-            out.append(acc)
-        return out
-
+                    windows[side][n].append(jnp.where(low_half, first, second))
     copies = []
     for side in range(2):
-        keys = [(img, k) for img, k, _ in windows[side]]
-        xs = band_pass([w for _, _, w in windows[side]], side, 0)
-        done = dict(zip(keys, xs))
-        deeper = [key for key in keys if key[1] >= 4]
-        done.update(zip(deeper, band_pass([done[key] for key in deeper], side, 1)))
-        deepest = [key for key in keys if key[1] >= 6]
-        done.update(zip(deepest, band_pass([done[key] for key in deepest], side, 2)))
+        outs = []
+        for n in range(3):
+            x = jnp.concatenate(windows[side][n], axis=0)
+            y = _dot(jnp.concatenate(_split(x), axis=1), w_ref[which[side], n])
+            outs.append(y[:, :LANES] + y[:, LANES:])
         inside = lane < PATCH if side == 0 else lane >= LANES - PATCH
         for img in range(IMAGES):
             t = side * IMAGES + img
             for q in range(4):
-                new = done[img, q]
+                at = (img * 4 + q) * 8
+                new = outs[0][at : at + 8]
                 if q < 2:
-                    new = jnp.where((lane & 1) == 0, done[img, 4 + q], new)
+                    at = (img * 2 + q) * 8
+                    new = jnp.where((lane & 1) == 0, outs[1][at : at + 8], new)
                 if q < 1:
-                    new = jnp.where((lane & 3) == 0, done[img, 6], new)
+                    new = jnp.where((lane & 3) == 0, outs[2][img * 8 : img * 8 + 8], new)
                 where = (t, pl.ds(OFFSETS[q], 8, stride=4), slice(None))
                 scr[where] = jnp.where(inside, pltpu.roll(new, HALF, 1), edge_in[where])
             for rt in range(4):
@@ -481,17 +507,17 @@
     out, out_edge = pl.pallas_call(
         main_kernel,
         out_shape=(shape(IMAGES, 4, CHUNKS, 8, LANES), held(EDGES, ROWS, LANES)),
-        in_specs=[VMEM] * 5,
+        in_specs=[VMEM] * 6,
         out_specs=(ANY, VMEM),
         scratch_shapes=[
             pltpu.VMEM((TILES, ROWS, LANES), F32),
-            pltpu.VMEM((7, CHUNKS, 8, LANES), F32),
+            *(pltpu.VMEM((CHUNKS * n, 2 * LANES), jnp.bfloat16) for n in (64, 64, 32, 32, 16, 16)),
             pltpu.VMEM((12 * TILES, LANES), F32),
             dma((IMAGES, 4)),
         ],
         cost_estimate=pl.CostEstimate(flops=40_000_000, transcendentals=0, bytes_accessed=2_000_000),
         name="interior",
-    )(*rows)
+    )(near(jnp.asarray(LINE)), *rows)
     out = pl.pallas_call(
         patch_kernel,
         out_shape=shape(IMAGES, 4, CHUNKS, 8, LANES),
@@ -500,7 +526,7 @@
         input_output_aliases={5: 0},
         scratch_shapes=[pltpu.VMEM((EDGES, ROWS, LANES), F32), dma((EDGES, 4))],
         name="edge_columns",
-    )(near(jnp.asarray(EDGE_TAPS)), near(v_edge), near(out_edge), halo_even, halo_odd, out)
+    )(near(jnp.asarray(EDGE)), near(v_edge), near(out_edge), halo_even, halo_odd, out)
     return out.transpose(0, 1, 3, 2, 4).reshape(IMAGES, ROWS, CHUNKS * LANES)
 
 

time: 28.2 us -> 24.6 us (0.87)
  the two profiles are of different devices: /device:TPU:7 before, /device:TPU:15 now
where the time goes in v4:
time: 24.6 us; the launch traced here: 24.4 us
  starting transfers between devices  12.6 us (51%)
  Pallas kernels  6.62 us (27%)
  waiting for transfers between devices  3.86 us (16%)
  local copies, waits for them, and re-layouts  1.27 us (5%)
    ppermute x2, starting transfers between devices, swap(): via_odd = lax.ppermute(odd, axis, odd_pairs)  9.93 us
    ppermute x2, waiting for transfers between devices, swap(): via_odd = lax.ppermute(odd, axis, odd_pairs)  3.86 us
    pallas_call x1, Pallas kernels, transform(): pl.pallas_call(main_kernel, out_shape=(shape(IMAGES, 4, CHUNKS, 8, LANES)...  3.02 us
    ppermute x2, starting transfers between devices, swap(): via_even = lax.ppermute(even, axis, even_pairs)  2.66 us
    pallas_call x1, Pallas kernels, transform(): pl.pallas_call(states_kernel, out_shape=(held(6 * TILES, LANES), held(6 *...  2.07 us
    pallas_call x1, Pallas kernels, transform(): pl.pallas_call(patch_kernel, out_shape=shape(IMAGES, 4, CHUNKS, 8, LANES)...  1.32 us
    unnamed x4, local copies, waits for them, and re-layouts  1.27 us
  transfers between devices with their start and end apart: 4, of which 1 were waited for; matrix products, arithmetic and copies ran while one was open for 0% of the time, Pallas kernels for 12%

profile of v4, /device:TPU:15, one launch (start us, length us, event | category | flops | bytes accessed | tf_op | source)
XLA Modules:
  0.0 24.4 jit_solution(5378997072687612315)
XLA Ops:
  0.0 2.1 %row_states.1 = (f32[384,128]{1,0:T(8,128)S(1)}, f32[384,128]{1,0:T(8,128)S(1)}, f32[64,32,128]{2,1,0:T(8,128)S(1)}) custom-call(f32[4,4,16,8,128]{4,3,2,1,0:T(8,128)} %bitcast.6), custom_call_target="tpu_custom_call" | custom-call | tf_op jit(solution)/shard_map/row_states/pallas_call | solution.py:488
  2.1 0.0 copy-start.1
  2.1 1.0 %collective-permute-start = (f32[384,128]{1,0:T(8,128)S(1)}, f32[384,128]{1,0:T(8,128)S(1)}, u32[]{:S(2)}, u32[]{:S(2)}) collective-permute-start(f32[384,128]{1,0:T(8,128)S(1)} %get-tuple-element.14.own_even), channel_id=1, source_target_pairs={{0,32},{32,0},{64,96},{96,64},{128,160},{160,128},{192,224},{224,1... | collective-permute-start | bytes 589832 | tf_op jit(solution)/shard_map/ppermute | solution.py:465
  3.0 3.1 %collective-permute-start.1 = (f32[384,128]{1,0:T(8,128)S(1)}, f32[384,128]{1,0:T(8,128)S(1)}, u32[]{:S(2)}, u32[]{:S(2)}) collective-permute-start(f32[384,128]{1,0:T(8,128)S(1)} %get-tuple-element.15.own_odd), channel_id=1, source_target_pairs={{32,64},{64,32},{96,128},{128,96},{160,192},{192,160},{0,0},{224,2... | collective-permute-start | bytes 589832 | tf_op jit(solution)/shard_map/ppermute | solution.py:464
  6.2 0.0 collective-permute-done.got_even
  6.2 3.9 %collective-permute-done.1.got_odd = f32[384,128]{1,0:T(8,128)S(1)} collective-permute-done((f32[384,128]{1,0:T(8,128)S(1)}, f32[384,128]{1,0:T(8,128)S(1)}, u32[]{:S(2)}, u32[]{:S(2)}) %collective-permute-start.1) | collective-permute-done | bytes 196640 | tf_op jit(solution)/shard_map/ppermute | solution.py:464
  10.0 0.2 edge_rows.1
  10.2 1.7 %collective-permute-start.2 = (f32[24,128]{1,0:T(8,128)S(1)}, f32[24,128]{1,0:T(8,128)S(1)}, u32[]{:S(2)}, u32[]{:S(2)}) collective-permute-start(f32[24,128]{1,0:T(8,128)S(1)} %get-tuple-element.18), channel_id=1, source_target_pairs={{0,1},{1,0},{2,3},{3,2},{4,5},{5,4},{6,7},{7,6},{8,9},{9,8},{10,11... | collective-permute-start | bytes 36872 | tf_op jit(solution)/shard_map/ppermute | solution.py:465
  12.0 6.8 %collective-permute-start.3 = (f32[24,128]{1,0:T(8,128)S(1)}, f32[24,128]{1,0:T(8,128)S(1)}, u32[]{:S(2)}, u32[]{:S(2)}) collective-permute-start(f32[24,128]{1,0:T(8,128)S(1)} %get-tuple-element.19), channel_id=1, source_target_pairs={{1,2},{2,1},{3,4},{4,3},{5,6},{6,5},{7,8},{8,7},{9,10},{10,9},{11,... | collective-permute-start | bytes 36872 | tf_op jit(solution)/shard_map/ppermute | solution.py:464
  18.8 0.0 copy-done.1
  18.8 3.0 %interior.1 = (f32[4,4,16,8,128]{4,3,2,1,0:T(8,128)}, f32[8,32,128]{2,1,0:T(8,128)S(1)}) custom-call(bf16[3,256,256]{2,1,0:T(8,128)(2,1)S(1)} %copy-done.1, f32[64,32,128]{2,1,0:T(8,128)S(1)} %get-tuple-element.13.x_ref, f32[384,128]{1,0:T(8,128)S(1)} %get-tuple-element.14.own_even, f32[384,128]{1,0:T(8,128)S(1)} %get-tuple-element.15.own_odd, ...), custom_call_target="tpu_custom_call" | custom-call | flops 40000000 | bytes 2000000 | tf_op jit(solution)/shard_map/interior/pallas_call | solution.py:507
  21.8 0.0 collective-permute-done.2.got_even
  21.8 0.0 collective-permute-done.3.got_odd
  21.8 0.0 copy-start
  21.9 1.3 %copy-done = bf16[3,3,256,256]{3,2,1,0:T(8,128)(2,1)S(1)} copy-done((bf16[3,3,256,256]{3,2,1,0:T(8,128)(2,1)S(1)}, bf16[3,3,256,256]{3,2,1,0:T(8,128)(2,1)}, u32[]{:S(2)}) %copy-start) | copy-done | bytes 1179672
  23.1 1.3 %edge_columns.1 = f32[4,4,16,8,128]{4,3,2,1,0:T(8,128)} custom-call(bf16[3,3,256,256]{3,2,1,0:T(8,128)(2,1)S(1)} %copy-done, f32[8,7,8,128]{3,2,1,0:T(8,128)S(1)} %get-tuple-element.16.v_ref, f32[8,32,128]{2,1,0:T(8,128)S(1)} %get-tuple-element.17.edge_in, f32[24,128]{1,0:T(8,128)S(1)} %collective-permute-done.2.got_even, ...), custom_call_target="tpu_custom_call", output_to_operand_aliasing={{}: (5, {})} | custom-call | tf_op jit(solution)/shard_map/edge_columns/pallas_call | solution.py:521
Async XLA Ops:
  2.1 16.7 %copy-start.1 = (bf16[3,256,256]{2,1,0:T(8,128)(2,1)S(1)}, bf16[3,256,256]{2,1,0:T(8,128)(2,1)}, u32[]{:S(2)}) copy-start(bf16[3,256,256]{2,1,0:T(8,128)(2,1)} %constant.4.clone.w_ref) | copy-start | bytes 1179652
  2.1 4.1 %collective-permute-start = (f32[384,128]{1,0:T(8,128)S(1)}, f32[384,128]{1,0:T(8,128)S(1)}, u32[]{:S(2)}, u32[]{:S(2)}) collective-permute-start(f32[384,128]{1,0:T(8,128)S(1)} %get-tuple-element.14.own_even), channel_id=1, source_target_pairs={{0,32},{32,0},{64,96},{96,64},{128,160},{160,128},{192,224},{224,1... | collective-permute-start | bytes 589832 | tf_op jit(solution)/shard_map/ppermute | solution.py:465
  3.0 7.0 %collective-permute-start.1 = (f32[384,128]{1,0:T(8,128)S(1)}, f32[384,128]{1,0:T(8,128)S(1)}, u32[]{:S(2)}, u32[]{:S(2)}) collective-permute-start(f32[384,128]{1,0:T(8,128)S(1)} %get-tuple-element.15.own_odd), channel_id=1, source_target_pairs={{32,64},{64,32},{96,128},{128,96},{160,192},{192,160},{0,0},{224,2... | collective-permute-start | bytes 589832 | tf_op jit(solution)/shard_map/ppermute | solution.py:464
  10.2 11.6 %collective-permute-start.2 = (f32[24,128]{1,0:T(8,128)S(1)}, f32[24,128]{1,0:T(8,128)S(1)}, u32[]{:S(2)}, u32[]{:S(2)}) collective-permute-start(f32[24,128]{1,0:T(8,128)S(1)} %get-tuple-element.18), channel_id=1, source_target_pairs={{0,1},{1,0},{2,3},{3,2},{4,5},{5,4},{6,7},{7,6},{8,9},{9,8},{10,11... | collective-permute-start | bytes 36872 | tf_op jit(solution)/shard_map/ppermute | solution.py:465
  12.0 9.9 %collective-permute-start.3 = (f32[24,128]{1,0:T(8,128)S(1)}, f32[24,128]{1,0:T(8,128)S(1)}, u32[]{:S(2)}, u32[]{:S(2)}) collective-permute-start(f32[24,128]{1,0:T(8,128)S(1)} %get-tuple-element.19), channel_id=1, source_target_pairs={{1,2},{2,1},{3,4},{4,3},{5,6},{6,5},{7,8},{8,7},{9,10},{10,9},{11,... | collective-permute-start | bytes 36872 | tf_op jit(solution)/shard_map/ppermute | solution.py:464
  21.8 1.3 %copy-start = (bf16[3,3,256,256]{3,2,1,0:T(8,128)(2,1)S(1)}, bf16[3,3,256,256]{3,2,1,0:T(8,128)(2,1)}, u32[]{:S(2)}) copy-start(bf16[3,3,256,256]{3,2,1,0:T(8,128)(2,1)} %constant.5.clone.w_ref) | copy-start | bytes 3538948

commit v5 on v4

--- a/solution.py
+++ b/solution.py
@@ -334,7 +334,8 @@
     return jnp.dot(x, w, preferred_element_type=F32)
 
 
-def main_kernel(w_ref, x_ref, own_even, own_odd, got_even, got_odd, out_ref, edge_ref, scr, lh1, ll1, lh2, ll2, lh3, ll3, bnd, sems):
+def main_kernel(later_ref, w_ref, x_ref, own_even, own_odd, got_even, got_odd, out_ref, edge_ref, scr, lh1, ll1, lh2, ll2, lh3, ll3, bnd, sems):
+    del later_ref
     _boundaries(own_even, own_odd, got_even, got_odd, bnd, TILES)
     lane = _lane()
     low_half = lane < HALF
@@ -445,14 +446,8 @@
                     new = jnp.where((lane & 3) == 0, outs[2][img * 8 : img * 8 + 8], new)
                 where = (t, pl.ds(OFFSETS[q], 8, stride=4), slice(None))
                 scr[where] = jnp.where(inside, pltpu.roll(new, HALF, 1), edge_in[where])
-            for rt in range(4):
-                copies.append(
-                    _load(
-                        scr.at[t, pl.ds(rt * 8, 8), :],
-                        out_ref.at[img, rt, (CHUNKS - 1) * side],
-                        sems.at[t, rt],
-                    )
-                )
+            column = scr.reshape(EDGES, 4, 8, LANES).at[t]
+            copies.append(_load(column, out_ref.at[img, :, (CHUNKS - 1) * side], sems.at[t]))
     for copy in copies:
         copy.wait()
 
@@ -491,8 +486,9 @@
         in_specs=[ANY],
         out_specs=(VMEM,) * 3,
         scratch_shapes=[dma((IMAGES, 4))],
+        compiler_params=pltpu.CompilerParams(vmem_limit_bytes=8 << 20),
         name="row_states",
-    )(x)
+    )(pltpu.with_memory_space_constraint(x, pltpu.HBM))
     got_even, got_odd = swap("row", row_even, row_odd)
     rows = (near(block), near(row_even), near(row_odd), got_even, got_odd)
     v_edge, col_even, col_odd = pl.pallas_call(
@@ -501,13 +497,15 @@
         in_specs=[VMEM] * 5,
         out_specs=(VMEM,) * 3,
         scratch_shapes=[pltpu.VMEM((12 * EDGES, LANES), F32)],
+        compiler_params=pltpu.CompilerParams(vmem_limit_bytes=8 << 20),
         name="edge_rows",
     )(*rows)
+    edge_matrices = near(jnp.asarray(EDGE))
     halo_even, halo_odd = swap("col", col_even, col_odd)
     out, out_edge = pl.pallas_call(
         main_kernel,
         out_shape=(shape(IMAGES, 4, CHUNKS, 8, LANES), held(EDGES, ROWS, LANES)),
-        in_specs=[VMEM] * 6,
+        in_specs=[VMEM] * 7,
         out_specs=(ANY, VMEM),
         scratch_shapes=[
             pltpu.VMEM((TILES, ROWS, LANES), F32),
@@ -516,17 +514,19 @@
             dma((IMAGES, 4)),
         ],
         cost_estimate=pl.CostEstimate(flops=40_000_000, transcendentals=0, bytes_accessed=2_000_000),
+        compiler_params=pltpu.CompilerParams(vmem_limit_bytes=24 << 20),
         name="interior",
-    )(near(jnp.asarray(LINE)), *rows)
+    )(edge_matrices, near(jnp.asarray(LINE)), *rows)
     out = pl.pallas_call(
         patch_kernel,
         out_shape=shape(IMAGES, 4, CHUNKS, 8, LANES),
         in_specs=[VMEM] * 5 + [ANY],
         out_specs=ANY,
         input_output_aliases={5: 0},
-        scratch_shapes=[pltpu.VMEM((EDGES, ROWS, LANES), F32), dma((EDGES, 4))],
+        scratch_shapes=[pltpu.VMEM((EDGES, ROWS, LANES), F32), dma((EDGES,))],
+        compiler_params=pltpu.CompilerParams(vmem_limit_bytes=8 << 20),
         name="edge_columns",
-    )(near(jnp.asarray(EDGE)), near(v_edge), near(out_edge), halo_even, halo_odd, out)
+    )(edge_matrices, near(v_edge), near(out_edge), halo_even, halo_odd, out)
     return out.transpose(0, 1, 3, 2, 4).reshape(IMAGES, ROWS, CHUNKS * LANES)
 
 

time: 24.6 us -> 23.2 us (0.943)
  the two profiles are of different devices: /device:TPU:15 before, /device:TPU:14 now
where the time goes in v5:
time: 23.2 us; the launch traced here: 23 us
  starting transfers between devices  11.6 us (50%)
  Pallas kernels  6.58 us (28%)
  waiting for transfers between devices  4.66 us (20%)
    ppermute x2, starting transfers between devices, swap(): via_odd = lax.ppermute(odd, axis, odd_pairs)  9.55 us
    ppermute x2, waiting for transfers between devices, swap(): via_odd = lax.ppermute(odd, axis, odd_pairs)  4.66 us
    pallas_call x1, Pallas kernels, transform(): pl.pallas_call(main_kernel, out_shape=(shape(IMAGES, 4, CHUNKS, 8, LANES)...  3.03 us
    pallas_call x1, Pallas kernels, transform(): pl.pallas_call(states_kernel, out_shape=(held(6 * TILES, LANES), held(6 *...  2.26 us
    ppermute x2, starting transfers between devices, swap(): via_even = lax.ppermute(even, axis, even_pairs)  2.08 us
    pallas_call x1, Pallas kernels, transform(): pl.pallas_call(patch_kernel, out_shape=shape(IMAGES, 4, CHUNKS, 8, LANES)...  1.07 us
  transfers between devices with their start and end apart: 4, of which 1 were waited for; matrix products, arithmetic and copies ran while one was open for 0% of the time, Pallas kernels for 13%

profile of v5, /device:TPU:14, one launch (start us, length us, event | category | flops | bytes accessed | tf_op | source)
XLA Modules:
  0.0 23.0 jit_solution(1073474064120074663)
XLA Ops:
  0.0 2.3 %row_states.1 = (f32[384,128]{1,0:T(8,128)S(1)}, f32[384,128]{1,0:T(8,128)S(1)}, f32[64,32,128]{2,1,0:T(8,128)S(1)}) custom-call(f32[4,4,16,8,128]{4,3,2,1,0:T(8,128)} %bitcast.6), custom_call_target="tpu_custom_call" | custom-call | tf_op jit(solution)/shard_map/row_states/pallas_call | solution.py:483
  2.3 0.0 copy-start
  2.3 0.0 copy-start.1
  2.3 0.1 collective-permute-start
  2.4 2.4 %collective-permute-start.1 = (f32[384,128]{1,0:T(8,128)S(1)}, f32[384,128]{1,0:T(8,128)S(1)}, u32[]{:S(2)}, u32[]{:S(2)}) collective-permute-start(f32[384,128]{1,0:T(8,128)S(1)} %get-tuple-element.15.own_odd), channel_id=1, source_target_pairs={{32,64},{64,32},{96,128},{128,96},{160,192},{192,160},{0,0},{224,2... | collective-permute-start | bytes 589832 | tf_op jit(solution)/shard_map/ppermute | solution.py:459
  4.9 0.0 collective-permute-done.got_even
  4.9 4.7 %collective-permute-done.1.got_odd = f32[384,128]{1,0:T(8,128)S(1)} collective-permute-done((f32[384,128]{1,0:T(8,128)S(1)}, f32[384,128]{1,0:T(8,128)S(1)}, u32[]{:S(2)}, u32[]{:S(2)}) %collective-permute-start.1) | collective-permute-done | bytes 196640 | tf_op jit(solution)/shard_map/ppermute | solution.py:459
  9.5 0.2 edge_rows.1
  9.7 2.0 %collective-permute-start.2 = (f32[24,128]{1,0:T(8,128)S(1)}, f32[24,128]{1,0:T(8,128)S(1)}, u32[]{:S(2)}, u32[]{:S(2)}) collective-permute-start(f32[24,128]{1,0:T(8,128)S(1)} %get-tuple-element.18), channel_id=1, source_target_pairs={{0,1},{1,0},{2,3},{3,2},{4,5},{5,4},{6,7},{7,6},{8,9},{9,8},{10,11... | collective-permute-start | bytes 36872 | tf_op jit(solution)/shard_map/ppermute | solution.py:460
  11.7 7.1 %collective-permute-start.3 = (f32[24,128]{1,0:T(8,128)S(1)}, f32[24,128]{1,0:T(8,128)S(1)}, u32[]{:S(2)}, u32[]{:S(2)}) collective-permute-start(f32[24,128]{1,0:T(8,128)S(1)} %get-tuple-element.19), channel_id=1, source_target_pairs={{1,2},{2,1},{3,4},{4,3},{5,6},{6,5},{7,8},{8,7},{9,10},{10,9},{11,... | collective-permute-start | bytes 36872 | tf_op jit(solution)/shard_map/ppermute | solution.py:459
  18.8 0.0 copy-done
  18.9 0.0 copy-done.1
  18.9 3.0 %interior.1 = (f32[4,4,16,8,128]{4,3,2,1,0:T(8,128)}, f32[8,32,128]{2,1,0:T(8,128)S(1)}) custom-call(bf16[3,3,256,256]{3,2,1,0:T(8,128)(2,1)S(1)} %copy-done, bf16[3,256,256]{2,1,0:T(8,128)(2,1)S(1)} %copy-done.1, f32[64,32,128]{2,1,0:T(8,128)S(1)} %get-tuple-element.13.x_ref, f32[384,128]{1,0:T(8,128)S(1)} %get-tuple-element.14.own_even, ...), custom_call_target="tpu_custom_call" | custom-call | flops 40000000 | bytes 2000000 | tf_op jit(solution)/shard_map/interior/pallas_call | solution.py:505
  21.9 0.0 collective-permute-done.2.got_even
  21.9 0.0 collective-permute-done.3.got_odd
  21.9 1.1 %edge_columns.1 = f32[4,4,16,8,128]{4,3,2,1,0:T(8,128)} custom-call(bf16[3,3,256,256]{3,2,1,0:T(8,128)(2,1)S(1)} %copy-done, f32[8,7,8,128]{3,2,1,0:T(8,128)S(1)} %get-tuple-element.16.v_ref, f32[8,32,128]{2,1,0:T(8,128)S(1)} %get-tuple-element.17.edge_in, f32[24,128]{1,0:T(8,128)S(1)} %collective-permute-done.2.got_even, ...), custom_call_target="tpu_custom_call", output_to_operand_aliasing={{}: (5, {})} | custom-call | tf_op jit(solution)/shard_map/edge_columns/pallas_call | solution.py:520
Async XLA Ops:
  2.3 16.6 %copy-start = (bf16[3,3,256,256]{3,2,1,0:T(8,128)(2,1)S(1)}, bf16[3,3,256,256]{3,2,1,0:T(8,128)(2,1)}, u32[]{:S(2)}) copy-start(bf16[3,3,256,256]{3,2,1,0:T(8,128)(2,1)} %constant.4.clone.later_ref.w_ref) | copy-start | bytes 3538948
  2.3 16.6 %copy-start.1 = (bf16[3,256,256]{2,1,0:T(8,128)(2,1)S(1)}, bf16[3,256,256]{2,1,0:T(8,128)(2,1)}, u32[]{:S(2)}) copy-start(bf16[3,256,256]{2,1,0:T(8,128)(2,1)} %constant.5.clone.w_ref) | copy-start | bytes 1179652
  2.3 2.6 %collective-permute-start = (f32[384,128]{1,0:T(8,128)S(1)}, f32[384,128]{1,0:T(8,128)S(1)}, u32[]{:S(2)}, u32[]{:S(2)}) collective-permute-start(f32[384,128]{1,0:T(8,128)S(1)} %get-tuple-element.14.own_even), channel_id=1, source_target_pairs={{0,32},{32,0},{64,96},{96,64},{128,160},{160,128},{192,224},{224,1... | collective-permute-start | bytes 589832 | tf_op jit(solution)/shard_map/ppermute | solution.py:460
  2.4 7.1 %collective-permute-start.1 = (f32[384,128]{1,0:T(8,128)S(1)}, f32[384,128]{1,0:T(8,128)S(1)}, u32[]{:S(2)}, u32[]{:S(2)}) collective-permute-start(f32[384,128]{1,0:T(8,128)S(1)} %get-tuple-element.15.own_odd), channel_id=1, source_target_pairs={{32,64},{64,32},{96,128},{128,96},{160,192},{192,160},{0,0},{224,2... | collective-permute-start | bytes 589832 | tf_op jit(solution)/shard_map/ppermute | solution.py:459
  9.7 12.2 %collective-permute-start.2 = (f32[24,128]{1,0:T(8,128)S(1)}, f32[24,128]{1,0:T(8,128)S(1)}, u32[]{:S(2)}, u32[]{:S(2)}) collective-permute-start(f32[24,128]{1,0:T(8,128)S(1)} %get-tuple-element.18), channel_id=1, source_target_pairs={{0,1},{1,0},{2,3},{3,2},{4,5},{5,4},{6,7},{7,6},{8,9},{9,8},{10,11... | collective-permute-start | bytes 36872 | tf_op jit(solution)/shard_map/ppermute | solution.py:460
  11.7 10.2 %collective-permute-start.3 = (f32[24,128]{1,0:T(8,128)S(1)}, f32[24,128]{1,0:T(8,128)S(1)}, u32[]{:S(2)}, u32[]{:S(2)}) collective-permute-start(f32[24,128]{1,0:T(8,128)S(1)} %get-tuple-element.19), channel_id=1, source_target_pairs={{1,2},{2,1},{3,4},{4,3},{5,6},{6,5},{7,8},{8,7},{9,10},{10,9},{11,... | collective-permute-start | bytes 36872 | tf_op jit(solution)/shard_map/ppermute | solution.py:459

commit v6 on v5

--- a/solution.py
+++ b/solution.py
@@ -273,23 +273,21 @@
         ]
         for img in range(IMAGES)
     ]
+
+    def run(to_end, to_start):
+        for img in range(IMAGES):
+            for copy in copies[img]:
+                copy.wait()
+            for c in range(CHUNKS):
+                t = tile_row(img, c)
+                end, start = _states_of(_rows_of(scr, img * CHUNKS + c))
+                for k in range(6):
+                    to_end[pl.ds(k * TILES + t, 1), :] = end[k]
+                    to_start[pl.ds(k * TILES + t, 1), :] = start[k]
+
     is_odd = lax.axis_index("row") % 2 == 1
-    for img in range(IMAGES):
-        for copy in copies[img]:
-            copy.wait()
-        for group in range(0, CHUNKS, 4):
-            got = [
-                (tile_row(img, c), *_states_of(_rows_of(scr, img * CHUNKS + c))) for c in range(group, group + 4)
-            ]
-
-            def put(to_end, to_start):
-                for t, end, start in got:
-                    for k in range(6):
-                        to_end[pl.ds(k * TILES + t, 1), :] = end[k]
-                        to_start[pl.ds(k * TILES + t, 1), :] = start[k]
-
-            pl.when(is_odd)(lambda: put(odd_ref, even_ref))
-            pl.when(jnp.logical_not(is_odd))(lambda: put(even_ref, odd_ref))
+    pl.when(is_odd)(lambda: run(odd_ref, even_ref))
+    pl.when(jnp.logical_not(is_odd))(lambda: run(even_ref, odd_ref))
 
 
 def edges_kernel(x_ref, own_even, own_odd, got_even, got_odd, v_ref, even_ref, odd_ref, bnd):

time: 23.2 us -> 22.8 us (0.983)
  Pallas kernels: 6.58 us -> 6.19 us
    pallas_call x1, Pallas kernels: 2.26 us -> 1.87 us  [transform(): pl.pallas_call(states_kernel, out_shape=(held(6 * TILES, LANES), held(6 *...]
where the time goes in v6:
time: 22.8 us; the launch traced here: 22.6 us
  starting transfers between devices  11.6 us (51%)
  Pallas kernels  6.19 us (27%)
  waiting for transfers between devices  4.66 us (20%)
    ppermute x2, starting transfers between devices, swap(): via_odd = lax.ppermute(odd, axis, odd_pairs)  9.55 us
    ppermute x2, waiting for transfers between devices, swap(): via_odd = lax.ppermute(odd, axis, odd_pairs)  4.66 us
    pallas_call x1, Pallas kernels, transform(): pl.pallas_call(main_kernel, out_shape=(shape(IMAGES, 4, CHUNKS, 8, LANES)...  3.02 us
    ppermute x2, starting transfers between devices, swap(): via_even = lax.ppermute(even, axis, even_pairs)  2.08 us
    pallas_call x1, Pallas kernels, transform(): pl.pallas_call(states_kernel, out_shape=(held(6 * TILES, LANES), held(6 *...  1.87 us
    pallas_call x1, Pallas kernels, transform(): pl.pallas_call(patch_kernel, out_shape=shape(IMAGES, 4, CHUNKS, 8, LANES)...  1.07 us
  transfers between devices with their start and end apart: 4, of which 1 were waited for; matrix products, arithmetic and copies ran while one was open for 0% of the time, Pallas kernels for 13%

profile of v6, /device:TPU:14, one launch (start us, length us, event | category | flops | bytes accessed | tf_op | source)
XLA Modules:
  0.0 22.6 jit_solution(10403594750593191790)
XLA Ops:
  0.0 1.9 %row_states.1 = (f32[384,128]{1,0:T(8,128)S(1)}, f32[384,128]{1,0:T(8,128)S(1)}, f32[64,32,128]{2,1,0:T(8,128)S(1)}) custom-call(f32[4,4,16,8,128]{4,3,2,1,0:T(8,128)} %bitcast.6), custom_call_target="tpu_custom_call" | custom-call | tf_op jit(solution)/shard_map/row_states/pallas_call | solution.py:481
  1.9 0.0 copy-start
  1.9 0.0 copy-start.1
  1.9 0.1 collective-permute-start
  2.0 2.4 %collective-permute-start.1 = (f32[384,128]{1,0:T(8,128)S(1)}, f32[384,128]{1,0:T(8,128)S(1)}, u32[]{:S(2)}, u32[]{:S(2)}) collective-permute-start(f32[384,128]{1,0:T(8,128)S(1)} %get-tuple-element.15.own_odd), channel_id=1, source_target_pairs={{32,64},{64,32},{96,128},{128,96},{160,192},{192,160},{0,0},{224,2... | collective-permute-start | bytes 589832 | tf_op jit(solution)/shard_map/ppermute | solution.py:457
  4.5 0.0 collective-permute-done.got_even
  4.5 4.7 %collective-permute-done.1.got_odd = f32[384,128]{1,0:T(8,128)S(1)} collective-permute-done((f32[384,128]{1,0:T(8,128)S(1)}, f32[384,128]{1,0:T(8,128)S(1)}, u32[]{:S(2)}, u32[]{:S(2)}) %collective-permute-start.1) | collective-permute-done | bytes 196640 | tf_op jit(solution)/shard_map/ppermute | solution.py:457
  9.1 0.2 edge_rows.1
  9.4 2.0 %collective-permute-start.2 = (f32[24,128]{1,0:T(8,128)S(1)}, f32[24,128]{1,0:T(8,128)S(1)}, u32[]{:S(2)}, u32[]{:S(2)}) collective-permute-start(f32[24,128]{1,0:T(8,128)S(1)} %get-tuple-element.18), channel_id=1, source_target_pairs={{0,1},{1,0},{2,3},{3,2},{4,5},{5,4},{6,7},{7,6},{8,9},{9,8},{10,11... | collective-permute-start | bytes 36872 | tf_op jit(solution)/shard_map/ppermute | solution.py:458
  11.3 7.1 %collective-permute-start.3 = (f32[24,128]{1,0:T(8,128)S(1)}, f32[24,128]{1,0:T(8,128)S(1)}, u32[]{:S(2)}, u32[]{:S(2)}) collective-permute-start(f32[24,128]{1,0:T(8,128)S(1)} %get-tuple-element.19), channel_id=1, source_target_pairs={{1,2},{2,1},{3,4},{4,3},{5,6},{6,5},{7,8},{8,7},{9,10},{10,9},{11,... | collective-permute-start | bytes 36872 | tf_op jit(solution)/shard_map/ppermute | solution.py:457
  18.5 0.0 copy-done
  18.5 0.0 copy-done.1
  18.5 3.0 %interior.1 = (f32[4,4,16,8,128]{4,3,2,1,0:T(8,128)}, f32[8,32,128]{2,1,0:T(8,128)S(1)}) custom-call(bf16[3,3,256,256]{3,2,1,0:T(8,128)(2,1)S(1)} %copy-done, bf16[3,256,256]{2,1,0:T(8,128)(2,1)S(1)} %copy-done.1, f32[64,32,128]{2,1,0:T(8,128)S(1)} %get-tuple-element.13.x_ref, f32[384,128]{1,0:T(8,128)S(1)} %get-tuple-element.14.own_even, ...), custom_call_target="tpu_custom_call" | custom-call | flops 40000000 | bytes 2000000 | tf_op jit(solution)/shard_map/interior/pallas_call | solution.py:503
  21.5 0.0 collective-permute-done.2.got_even
  21.5 0.0 collective-permute-done.3.got_odd
  21.5 1.1 %edge_columns.1 = f32[4,4,16,8,128]{4,3,2,1,0:T(8,128)} custom-call(bf16[3,3,256,256]{3,2,1,0:T(8,128)(2,1)S(1)} %copy-done, f32[8,7,8,128]{3,2,1,0:T(8,128)S(1)} %get-tuple-element.16.v_ref, f32[8,32,128]{2,1,0:T(8,128)S(1)} %get-tuple-element.17.edge_in, f32[24,128]{1,0:T(8,128)S(1)} %collective-permute-done.2.got_even, ...), custom_call_target="tpu_custom_call", output_to_operand_aliasing={{}: (5, {})} | custom-call | tf_op jit(solution)/shard_map/edge_columns/pallas_call | solution.py:518
Async XLA Ops:
  1.9 16.6 %copy-start = (bf16[3,3,256,256]{3,2,1,0:T(8,128)(2,1)S(1)}, bf16[3,3,256,256]{3,2,1,0:T(8,128)(2,1)}, u32[]{:S(2)}) copy-start(bf16[3,3,256,256]{3,2,1,0:T(8,128)(2,1)} %constant.4.clone.later_ref.w_ref) | copy-start | bytes 3538948
  1.9 16.6 %copy-start.1 = (bf16[3,256,256]{2,1,0:T(8,128)(2,1)S(1)}, bf16[3,256,256]{2,1,0:T(8,128)(2,1)}, u32[]{:S(2)}) copy-start(bf16[3,256,256]{2,1,0:T(8,128)(2,1)} %constant.5.clone.w_ref) | copy-start | bytes 1179652
  1.9 2.6 %collective-permute-start = (f32[384,128]{1,0:T(8,128)S(1)}, f32[384,128]{1,0:T(8,128)S(1)}, u32[]{:S(2)}, u32[]{:S(2)}) collective-permute-start(f32[384,128]{1,0:T(8,128)S(1)} %get-tuple-element.14.own_even), channel_id=1, source_target_pairs={{0,32},{32,0},{64,96},{96,64},{128,160},{160,128},{192,224},{224,1... | collective-permute-start | bytes 589832 | tf_op jit(solution)/shard_map/ppermute | solution.py:458
  2.0 7.1 %collective-permute-start.1 = (f32[384,128]{1,0:T(8,128)S(1)}, f32[384,128]{1,0:T(8,128)S(1)}, u32[]{:S(2)}, u32[]{:S(2)}) collective-permute-start(f32[384,128]{1,0:T(8,128)S(1)} %get-tuple-element.15.own_odd), channel_id=1, source_target_pairs={{32,64},{64,32},{96,128},{128,96},{160,192},{192,160},{0,0},{224,2... | collective-permute-start | bytes 589832 | tf_op jit(solution)/shard_map/ppermute | solution.py:457
  9.4 12.2 %collective-permute-start.2 = (f32[24,128]{1,0:T(8,128)S(1)}, f32[24,128]{1,0:T(8,128)S(1)}, u32[]{:S(2)}, u32[]{:S(2)}) collective-permute-start(f32[24,128]{1,0:T(8,128)S(1)} %get-tuple-element.18), channel_id=1, source_target_pairs={{0,1},{1,0},{2,3},{3,2},{4,5},{5,4},{6,7},{7,6},{8,9},{9,8},{10,11... | collective-permute-start | bytes 36872 | tf_op jit(solution)/shard_map/ppermute | solution.py:458
  11.3 10.2 %collective-permute-start.3 = (f32[24,128]{1,0:T(8,128)S(1)}, f32[24,128]{1,0:T(8,128)S(1)}, u32[]{:S(2)}, u32[]{:S(2)}) collective-permute-start(f32[24,128]{1,0:T(8,128)S(1)} %get-tuple-element.19), channel_id=1, source_target_pairs={{1,2},{2,1},{3,4},{4,3},{5,6},{6,5},{7,8},{8,7},{9,10},{10,9},{11,... | collective-permute-start | bytes 36872 | tf_op jit(solution)/shard_map/ppermute | solution.py:457

commit v7 on v6

--- a/solution.py
+++ b/solution.py
@@ -332,7 +332,7 @@
     return jnp.dot(x, w, preferred_element_type=F32)
 
 
-def main_kernel(later_ref, w_ref, x_ref, own_even, own_odd, got_even, got_odd, out_ref, edge_ref, scr, lh1, ll1, lh2, ll2, lh3, ll3, bnd, sems):
+def interior(pairs, later_ref, w_ref, x_ref, own_even, own_odd, got_even, got_odd, edge_ref, scr, lh1, ll1, lh2, ll2, lh3, ll3, bnd, done):
     del later_ref
     _boundaries(own_even, own_odd, got_even, got_odd, bnd, TILES)
     lane = _lane()
@@ -386,23 +386,47 @@
                         val = jnp.where((lane & 3) == 0, outs[2][at : at + 8], val)
                     scr[img * CHUNKS + c, pl.ds(OFFSETS[q], 8, stride=4), :] = val
 
-    stores = []
-    for pair in ((0, 1), (2, 3)):
+    for pair in pairs:
         build(pair)
         multiply(pair)
         for img in pair:
             for side, chunk in enumerate((0, CHUNKS - 1)):
                 edge_ref[side * IMAGES + img] = scr[img * CHUNKS + chunk]
-            for rt in range(4):
-                stores.append(
-                    _load(
-                        scr.at[pl.ds(img * CHUNKS + 1, CHUNKS - 2), pl.ds(rt * 8, 8), :],
-                        out_ref.at[img, rt, pl.ds(1, CHUNKS - 2)],
-                        sems.at[img, rt],
-                    )
-                )
-    for copy in stores:
-        copy.wait()
+        done(pair)
+
+
+def is_early():
+    return lax.axis_index("col") % 8 == 0
+
+
+FIRST, SECOND = (0, 1), (2, 3)
+
+
+def early_kernel(*refs):
+    pl.when(is_early())(lambda: interior((FIRST,), *refs, lambda pair: None))
+
+
+def late_kernel(*refs):
+    ins, (_, kept, out_ref, edge_ref, scr, *rest, sems) = refs[:7], refs[7:]
+
+    def store(pair, source):
+        return [
+            _load(
+                source.at[pl.ds(img * CHUNKS + 1, CHUNKS - 2), pl.ds(rt * 8, 8), :],
+                out_ref.at[img, rt, pl.ds(1, CHUNKS - 2)],
+                sems.at[img, rt],
+            )
+            for img in pair
+            for rt in range(4)
+        ]
+
+    def run(pairs, stores):
+        interior(pairs, *ins, edge_ref, scr, *rest, lambda pair: stores.extend(store(pair, scr)))
+        for copy in stores:
+            copy.wait()
+
+    pl.when(is_early())(lambda: run((SECOND,), store(FIRST, kept)))
+    pl.when(jnp.logical_not(is_early()))(lambda: run((FIRST, SECOND), []))
 
 
 def patch_kernel(w_ref, v_ref, edge_in, got_even, got_odd, dest_ref, out_ref, scr, sems):
@@ -450,10 +474,15 @@
         copy.wait()
 
 
-def swap(axis, even, odd):
+def pairs(axis):
     n = lax.axis_size(axis)
     even_pairs = [(i, i ^ 1) for i in range(n)]
     odd_pairs = [(i, i + 1 if i % 2 else i - 1) for i in range(1, n - 1)] + [(0, 0), (n - 1, n - 1)]
+    return even_pairs, odd_pairs
+
+
+def swap(axis, even, odd):
+    even_pairs, odd_pairs = pairs(axis)
     via_odd = lax.ppermute(odd, axis, odd_pairs)
     via_even = lax.ppermute(even, axis, even_pairs)
     return near(via_even), near(via_odd)
@@ -499,22 +528,39 @@
         name="edge_rows",
     )(*rows)
     edge_matrices = near(jnp.asarray(EDGE))
-    halo_even, halo_odd = swap("col", col_even, col_odd)
-    out, out_edge = pl.pallas_call(
-        main_kernel,
-        out_shape=(shape(IMAGES, 4, CHUNKS, 8, LANES), held(EDGES, ROWS, LANES)),
-        in_specs=[VMEM] * 7,
-        out_specs=(ANY, VMEM),
-        scratch_shapes=[
-            pltpu.VMEM((TILES, ROWS, LANES), F32),
-            *(pltpu.VMEM((CHUNKS * n, 2 * LANES), jnp.bfloat16) for n in (64, 64, 32, 32, 16, 16)),
-            pltpu.VMEM((12 * TILES, LANES), F32),
-            dma((IMAGES, 4)),
-        ],
+    operands = (edge_matrices, near(jnp.asarray(LINE)), *rows)
+    work = [
+        *(pltpu.VMEM((CHUNKS * n, 2 * LANES), jnp.bfloat16) for n in (64, 64, 32, 32, 16, 16)),
+        pltpu.VMEM((12 * TILES, LANES), F32),
+    ]
+    settings = dict(
         cost_estimate=pl.CostEstimate(flops=40_000_000, transcendentals=0, bytes_accessed=2_000_000),
         compiler_params=pltpu.CompilerParams(vmem_limit_bytes=24 << 20),
-        name="interior",
-    )(edge_matrices, near(jnp.asarray(LINE)), *rows)
+    )
+    even_pairs, odd_pairs = pairs("col")
+    halo_even = lax.ppermute(col_even, "col", even_pairs)
+    out_edge, kept = pl.pallas_call(
+        early_kernel,
+        out_shape=(held(EDGES, ROWS, LANES), held(TILES, ROWS, LANES)),
+        in_specs=[VMEM] * 7,
+        out_specs=(VMEM, VMEM),
+        scratch_shapes=work,
+        name="interior_early",
+        **settings,
+    )(*operands)
+    col_odd, out_edge = lax.optimization_barrier((col_odd, out_edge))
+    halo_odd = lax.ppermute(near(col_odd), "col", odd_pairs)
+    out, out_edge = pl.pallas_call(
+        late_kernel,
+        out_shape=(shape(IMAGES, 4, CHUNKS, 8, LANES), held(EDGES, ROWS, LANES)),
+        in_specs=[VMEM] * 9,
+        out_specs=(ANY, VMEM),
+        input_output_aliases={7: 1},
+        scratch_shapes=[pltpu.VMEM((TILES, ROWS, LANES), F32), *work, dma((IMAGES, 4))],
+        name="interior_late",
+        **settings,
+    )(*operands, near(out_edge), near(kept))
+    halo_even, halo_odd = near(halo_even), near(halo_odd)
     out = pl.pallas_call(
         patch_kernel,
         out_shape=shape(IMAGES, 4, CHUNKS, 8, LANES),

time: 22.8 us -> 21.9 us (0.961)
  starting transfers between devices: 11.6 us -> 10.4 us
  Pallas kernels: 6.19 us -> 6.56 us
    ppermute x0 -> x2, starting transfers between devices: none -> 7.85 us  [the longest x1 5.87 us: transform(): halo_odd = lax.ppermute(near(col_odd), 'col', odd_pairs)]
    ppermute x2 -> x1, starting transfers between devices: 9.55 us -> 2.45 us  [swap(): via_odd = lax.ppermute(odd, axis, odd_pairs)]
    ppermute x2 -> x1, starting transfers between devices: 2.08 us -> 0.09 us  [swap(): via_even = lax.ppermute(even, axis, even_pairs)]
    pallas_call x1 -> x2, Pallas kernels: 3.02 us -> 3.39 us  [the longest x1 2.15 us: transform(): pl.pallas_call(late_kernel, out_shape=(shape(IMAGES, 4, CHUNKS, 8, LANES)...]
    ppermute x2 -> x1, waiting for transfers between devices: 4.66 us -> 4.65 us  [swap(): via_odd = lax.ppermute(odd, axis, odd_pairs)]
  transfers between devices with their start and end apart: 4 -> 4, of which waited for: 1 -> 1; matrix products, arithmetic and copies ran while one was open for 0% -> 0% of each run, Pallas kernels for 13% -> 16%
where the time goes in v7:
time: 21.9 us; the launch traced here: 21.7 us
  starting transfers between devices  10.4 us (47%)
  Pallas kernels  6.56 us (30%)
  waiting for transfers between devices  4.66 us (21%)
    ppermute x1, starting transfers between devices, transform(): halo_odd = lax.ppermute(near(col_odd), 'col', odd_pairs)  5.87 us
    ppermute x1, waiting for transfers between devices, swap(): via_odd = lax.ppermute(odd, axis, odd_pairs)  4.65 us
    ppermute x1, starting transfers between devices, swap(): via_odd = lax.ppermute(odd, axis, odd_pairs)  2.45 us
    pallas_call x1, Pallas kernels, transform(): pl.pallas_call(late_kernel, out_shape=(shape(IMAGES, 4, CHUNKS, 8, LANES)...  2.15 us
    ppermute x1, starting transfers between devices, transform(): halo_even = lax.ppermute(col_even, 'col', even_pairs)  1.98 us
    pallas_call x1, Pallas kernels, transform(): pl.pallas_call(states_kernel, out_shape=(held(6 * TILES, LANES), held(6 *...  1.87 us
    pallas_call x1, Pallas kernels, transform(): pl.pallas_call(early_kernel, out_shape=(held(EDGES, ROWS, LANES), held(TI...  1.24 us
    pallas_call x1, Pallas kernels, transform(): pl.pallas_call(patch_kernel, out_shape=shape(IMAGES, 4, CHUNKS, 8, LANES)...  1.07 us
  transfers between devices with their start and end apart: 4, of which 1 were waited for; matrix products, arithmetic and copies ran while one was open for 0% of the time, Pallas kernels for 16%

profile of v7, /device:TPU:14, one launch (start us, length us, event | category | flops | bytes accessed | tf_op | source)
XLA Modules:
  0.0 21.7 jit_solution(12047872355025102811)
XLA Ops:
  0.0 1.9 %row_states.1 = (f32[384,128]{1,0:T(8,128)S(1)}, f32[384,128]{1,0:T(8,128)S(1)}, f32[64,32,128]{2,1,0:T(8,128)S(1)}) custom-call(f32[4,4,16,8,128]{4,3,2,1,0:T(8,128)} %bitcast.6), custom_call_target="tpu_custom_call" | custom-call | tf_op jit(solution)/shard_map/row_states/pallas_call | solution.py:510
  1.9 0.0 copy-start
  1.9 0.0 copy-start.1
  1.9 0.1 collective-permute-start
  2.0 2.4 %collective-permute-start.1 = (f32[384,128]{1,0:T(8,128)S(1)}, f32[384,128]{1,0:T(8,128)S(1)}, u32[]{:S(2)}, u32[]{:S(2)}) collective-permute-start(f32[384,128]{1,0:T(8,128)S(1)} %get-tuple-element.19.own_odd.refs_4_), channel_id=1, source_target_pairs={{32,64},{64,32},{96,128},{128,96},{160,192},{192,160},{0,0},{224,2... | collective-permute-start | bytes 589832 | tf_op jit(solution)/shard_map/ppermute | solution.py:486
  4.5 0.0 collective-permute-done.got_even.refs_5_
  4.5 4.7 %collective-permute-done.1.got_odd.refs_6_ = f32[384,128]{1,0:T(8,128)S(1)} collective-permute-done((f32[384,128]{1,0:T(8,128)S(1)}, f32[384,128]{1,0:T(8,128)S(1)}, u32[]{:S(2)}, u32[]{:S(2)}) %collective-permute-start.1) | collective-permute-done | bytes 196640 | tf_op jit(solution)/shard_map/ppermute | solution.py:486
  9.1 0.2 %edge_rows.1 = (f32[8,7,8,128]{3,2,1,0:T(8,128)S(1)}, f32[24,128]{1,0:T(8,128)S(1)}, f32[24,128]{1,0:T(8,128)S(1)}) custom-call(f32[64,32,128]{2,1,0:T(8,128)S(1)} %get-tuple-element.17.x_ref.refs_2_, f32[384,128]{1,0:T(8,128)S(1)} %get-tuple-element.18.own_even.refs_3_, f32[384,128]{1,0:T(8,128)S(1)} %get-tuple-element.19.own_odd.refs_4_, ...), custom_call_target="tpu_custom_call" | custom-call | tf_op jit(solution)/shard_map/edge_rows/pallas_call | solution.py:521
  9.4 2.0 %collective-permute-start.2 = (f32[24,128]{1,0:T(8,128)S(1)}, f32[24,128]{1,0:T(8,128)S(1)}, u32[]{:S(2)}, u32[]{:S(2)}) collective-permute-start(f32[24,128]{1,0:T(8,128)S(1)} %get-tuple-element.26), channel_id=1, source_target_pairs={{0,1},{1,0},{2,3},{3,2},{4,5},{5,4},{6,7},{7,6},{8,9},{9,8},{10,11... | collective-permute-start | bytes 36872 | tf_op jit(solution)/shard_map/ppermute | solution.py:541
  11.3 0.0 copy-done
  11.3 0.0 copy-done.1
  11.3 1.2 %interior_early.1 = (f32[8,32,128]{2,1,0:T(8,128)S(1)}, f32[64,32,128]{2,1,0:T(8,128)S(1)}) custom-call(bf16[3,3,256,256]{3,2,1,0:T(8,128)(2,1)S(1)} %copy-done, bf16[3,256,256]{2,1,0:T(8,128)(2,1)S(1)} %copy-done.1, f32[64,32,128]{2,1,0:T(8,128)S(1)} %get-tuple-element.17.x_ref.refs_2_, f32[384,128]{1,0:T(8,128)S(1)} %get-tuple-element.18.own_even.refs_3_, ...), custom_call_target="tpu_custom_call" | custom-call | flops 40000000 | bytes 2000000 | tf_op jit(solution)/shard_map/interior_early/pallas_call | solution.py:542
  12.6 5.9 %collective-permute-start.3 = (f32[24,128]{1,0:T(8,128)S(1)}, f32[24,128]{1,0:T(8,128)S(1)}, u32[]{:S(2)}, u32[]{:S(2)}) collective-permute-start(f32[24,128]{1,0:T(8,128)S(1)} %get-tuple-element.27), channel_id=1, source_target_pairs={{1,2},{2,1},{3,4},{4,3},{5,6},{6,5},{7,8},{8,7},{9,10},{10,9},{11,... | collective-permute-start | bytes 36872 | tf_op jit(solution)/shard_map/ppermute | solution.py:552
  18.5 2.2 %interior_late.1 = (f32[4,4,16,8,128]{4,3,2,1,0:T(8,128)}, f32[8,32,128]{2,1,0:T(8,128)S(1)}) custom-call(bf16[3,3,256,256]{3,2,1,0:T(8,128)(2,1)S(1)} %copy-done, bf16[3,256,256]{2,1,0:T(8,128)(2,1)S(1)} %copy-done.1, f32[64,32,128]{2,1,0:T(8,128)S(1)} %get-tuple-element.17.x_ref.refs_2_, ...), custom_call_target="tpu_custom_call", output_to_operand_aliasing={{1}: (7, {})} | custom-call | flops 40000000 | bytes 2000000 | tf_op jit(solution)/shard_map/interior_late/pallas_call | solution.py:553
  20.6 0.0 collective-permute-done.2.got_even
  20.6 0.0 collective-permute-done.3.got_odd
  20.6 1.1 %edge_columns.1 = f32[4,4,16,8,128]{4,3,2,1,0:T(8,128)} custom-call(bf16[3,3,256,256]{3,2,1,0:T(8,128)(2,1)S(1)} %copy-done, f32[8,7,8,128]{3,2,1,0:T(8,128)S(1)} %get-tuple-element.20.v_ref, f32[8,32,128]{2,1,0:T(8,128)S(1)} %get-tuple-element.25.edge_in, f32[24,128]{1,0:T(8,128)S(1)} %collective-permute-done.2.got_even, ...), custom_call_target="tpu_custom_call", output_to_operand_aliasing={{}: (5, {})} | custom-call | tf_op jit(solution)/shard_map/edge_columns/pallas_call | solution.py:564
Async XLA Ops:
  1.9 9.5 %copy-start = (bf16[3,3,256,256]{3,2,1,0:T(8,128)(2,1)S(1)}, bf16[3,3,256,256]{3,2,1,0:T(8,128)(2,1)}, u32[]{:S(2)}) copy-start(bf16[3,3,256,256]{3,2,1,0:T(8,128)(2,1)} %constant.4.clone.refs_0_.w_ref) | copy-start | bytes 3538948
  1.9 9.4 %copy-start.1 = (bf16[3,256,256]{2,1,0:T(8,128)(2,1)S(1)}, bf16[3,256,256]{2,1,0:T(8,128)(2,1)}, u32[]{:S(2)}) copy-start(bf16[3,256,256]{2,1,0:T(8,128)(2,1)} %constant.5.clone.refs_1_) | copy-start | bytes 1179652
  1.9 2.6 %collective-permute-start = (f32[384,128]{1,0:T(8,128)S(1)}, f32[384,128]{1,0:T(8,128)S(1)}, u32[]{:S(2)}, u32[]{:S(2)}) collective-permute-start(f32[384,128]{1,0:T(8,128)S(1)} %get-tuple-element.18.own_even.refs_3_), channel_id=1, source_target_pairs={{0,32},{32,0},{64,96},{96,64},{128,160},{160,128},{192,224},{224,1... | collective-permute-start | bytes 589832 | tf_op jit(solution)/shard_map/ppermute | solution.py:487
  2.0 7.1 %collective-permute-start.1 = (f32[384,128]{1,0:T(8,128)S(1)}, f32[384,128]{1,0:T(8,128)S(1)}, u32[]{:S(2)}, u32[]{:S(2)}) collective-permute-start(f32[384,128]{1,0:T(8,128)S(1)} %get-tuple-element.19.own_odd.refs_4_), channel_id=1, source_target_pairs={{32,64},{64,32},{96,128},{128,96},{160,192},{192,160},{0,0},{224,2... | collective-permute-start | bytes 589832 | tf_op jit(solution)/shard_map/ppermute | solution.py:486
  9.4 11.3 %collective-permute-start.2 = (f32[24,128]{1,0:T(8,128)S(1)}, f32[24,128]{1,0:T(8,128)S(1)}, u32[]{:S(2)}, u32[]{:S(2)}) collective-permute-start(f32[24,128]{1,0:T(8,128)S(1)} %get-tuple-element.26), channel_id=1, source_target_pairs={{0,1},{1,0},{2,3},{3,2},{4,5},{5,4},{6,7},{7,6},{8,9},{9,8},{10,11... | collective-permute-start | bytes 36872 | tf_op jit(solution)/shard_map/ppermute | solution.py:541
  12.6 8.0 %collective-permute-start.3 = (f32[24,128]{1,0:T(8,128)S(1)}, f32[24,128]{1,0:T(8,128)S(1)}, u32[]{:S(2)}, u32[]{:S(2)}) collective-permute-start(f32[24,128]{1,0:T(8,128)S(1)} %get-tuple-element.27), channel_id=1, source_target_pairs={{1,2},{2,1},{3,4},{4,3},{5,6},{6,5},{7,8},{8,7},{9,10},{10,9},{11,... | collective-permute-start | bytes 36872 | tf_op jit(solution)/shard_map/ppermute | solution.py:552

commit v8 on v7

--- a/solution.py
+++ b/solution.py
@@ -119,7 +119,8 @@
 def _edge_matrices():
     out = []
     for mirror in (None, (0, 2 * LANES), (1, 2 * LANES - 1)):
-        high, low = _parts(_matrices(4 * LANES, (2 * LANES - HALF, LANES), (2 * LANES - HALF, LANES), mirror))
+        table = _matrices(4 * LANES, (2 * LANES - HALF, LANES), (2 * LANES - HALF, LANES), mirror)
+        high, low = _parts(np.roll(table, (HALF, HALF), axis=(1, 2)))
         top = np.concatenate([high, low], axis=2)
         bottom = np.concatenate([high, np.zeros_like(high)], axis=2)
         out.append(np.concatenate([top, bottom], axis=1))
@@ -443,10 +444,10 @@
         for img in range(IMAGES):
             for q in range(count):
                 slot = (img * count + q) * width
-                for side, shift in ((0, HALF - slot - width), (1, HALF - slot)):
+                for side, shift in ((0, LANES - slot - width), (1, LANES - slot)):
                     halo = pltpu.roll(got[side], shift % LANES, 1) if shift % LANES else got[side]
-                    own = pltpu.roll(v_ref[side * IMAGES + img, base + q], HALF, 1)
-                    first, second = (halo, own) if side == 0 else (own, halo)
+                    own = v_ref[side * IMAGES + img, base + q]
+                    first, second = (own, halo) if side == 0 else (halo, own)
                     windows[side][n].append(jnp.where(low_half, first, second))
     copies = []
     for side in range(2):
@@ -467,7 +468,7 @@
                 if q < 1:
                     new = jnp.where((lane & 3) == 0, outs[2][img * 8 : img * 8 + 8], new)
                 where = (t, pl.ds(OFFSETS[q], 8, stride=4), slice(None))
-                scr[where] = jnp.where(inside, pltpu.roll(new, HALF, 1), edge_in[where])
+                scr[where] = jnp.where(inside, new, edge_in[where])
             column = scr.reshape(EDGES, 4, 8, LANES).at[t]
             copies.append(_load(column, out_ref.at[img, :, (CHUNKS - 1) * side], sems.at[t]))
     for copy in copies:

time: 21.9 us -> 21.8 us (level)
  the two profiles are of different devices: /device:TPU:14 before, /device:TPU:22 now
where the time goes in v8:
time: 21.8 us; the launch traced here: 21.6 us
  starting transfers between devices  10.4 us (48%)
  Pallas kernels  6.48 us (30%)
  waiting for transfers between devices  4.66 us (21%)
    ppermute x1, starting transfers between devices, transform(): halo_odd = lax.ppermute(near(col_odd), 'col', odd_pairs)  5.87 us
    ppermute x1, waiting for transfers between devices, swap(): via_odd = lax.ppermute(odd, axis, odd_pairs)  4.65 us
    ppermute x1, starting transfers between devices, swap(): via_odd = lax.ppermute(odd, axis, odd_pairs)  2.45 us
    pallas_call x1, Pallas kernels, transform(): pl.pallas_call(late_kernel, out_shape=(shape(IMAGES, 4, CHUNKS, 8, LANES)...  2.15 us
    ppermute x1, starting transfers between devices, transform(): halo_even = lax.ppermute(col_even, 'col', even_pairs)  1.98 us
    pallas_call x1, Pallas kernels, transform(): pl.pallas_call(states_kernel, out_shape=(held(6 * TILES, LANES), held(6 *...  1.87 us
    pallas_call x1, Pallas kernels, transform(): pl.pallas_call(early_kernel, out_shape=(held(EDGES, ROWS, LANES), held(TI...  1.24 us
    pallas_call x1, Pallas kernels, transform(): pl.pallas_call(patch_kernel, out_shape=shape(IMAGES, 4, CHUNKS, 8, LANES)...  0.99 us
  transfers between devices with their start and end apart: 4, of which 1 were waited for; matrix products, arithmetic and copies ran while one was open for 0% of the time, Pallas kernels for 16%

profile of v8, /device:TPU:22, one launch (start us, length us, event | category | flops | bytes accessed | tf_op | source)
XLA Modules:
  0.0 21.6 jit_solution(18140005082113963195)
XLA Ops:
  0.0 1.9 %row_states.1 = (f32[384,128]{1,0:T(8,128)S(1)}, f32[384,128]{1,0:T(8,128)S(1)}, f32[64,32,128]{2,1,0:T(8,128)S(1)}) custom-call(f32[4,4,16,8,128]{4,3,2,1,0:T(8,128)} %bitcast.6), custom_call_target="tpu_custom_call" | custom-call | tf_op jit(solution)/shard_map/row_states/pallas_call | solution.py:511
  1.9 0.0 copy-start
  1.9 0.0 copy-start.1
  1.9 0.1 collective-permute-start
  2.0 2.4 %collective-permute-start.1 = (f32[384,128]{1,0:T(8,128)S(1)}, f32[384,128]{1,0:T(8,128)S(1)}, u32[]{:S(2)}, u32[]{:S(2)}) collective-permute-start(f32[384,128]{1,0:T(8,128)S(1)} %get-tuple-element.19.own_odd.refs_4_), channel_id=1, source_target_pairs={{32,64},{64,32},{96,128},{128,96},{160,192},{192,160},{0,0},{224,2... | collective-permute-start | bytes 589832 | tf_op jit(solution)/shard_map/ppermute | solution.py:487
  4.5 0.0 collective-permute-done.got_even.refs_5_
  4.5 4.7 %collective-permute-done.1.got_odd.refs_6_ = f32[384,128]{1,0:T(8,128)S(1)} collective-permute-done((f32[384,128]{1,0:T(8,128)S(1)}, f32[384,128]{1,0:T(8,128)S(1)}, u32[]{:S(2)}, u32[]{:S(2)}) %collective-permute-start.1) | collective-permute-done | bytes 196640 | tf_op jit(solution)/shard_map/ppermute | solution.py:487
  9.1 0.2 %edge_rows.1 = (f32[8,7,8,128]{3,2,1,0:T(8,128)S(1)}, f32[24,128]{1,0:T(8,128)S(1)}, f32[24,128]{1,0:T(8,128)S(1)}) custom-call(f32[64,32,128]{2,1,0:T(8,128)S(1)} %get-tuple-element.17.x_ref.refs_2_, f32[384,128]{1,0:T(8,128)S(1)} %get-tuple-element.18.own_even.refs_3_, f32[384,128]{1,0:T(8,128)S(1)} %get-tuple-element.19.own_odd.refs_4_, ...), custom_call_target="tpu_custom_call" | custom-call | tf_op jit(solution)/shard_map/edge_rows/pallas_call | solution.py:522
  9.4 2.0 %collective-permute-start.2 = (f32[24,128]{1,0:T(8,128)S(1)}, f32[24,128]{1,0:T(8,128)S(1)}, u32[]{:S(2)}, u32[]{:S(2)}) collective-permute-start(f32[24,128]{1,0:T(8,128)S(1)} %get-tuple-element.26), channel_id=1, source_target_pairs={{0,1},{1,0},{2,3},{3,2},{4,5},{5,4},{6,7},{7,6},{8,9},{9,8},{10,11... | collective-permute-start | bytes 36872 | tf_op jit(solution)/shard_map/ppermute | solution.py:542
  11.3 0.0 copy-done
  11.3 0.0 copy-done.1
  11.3 1.2 %interior_early.1 = (f32[8,32,128]{2,1,0:T(8,128)S(1)}, f32[64,32,128]{2,1,0:T(8,128)S(1)}) custom-call(bf16[3,3,256,256]{3,2,1,0:T(8,128)(2,1)S(1)} %copy-done, bf16[3,256,256]{2,1,0:T(8,128)(2,1)S(1)} %copy-done.1, f32[64,32,128]{2,1,0:T(8,128)S(1)} %get-tuple-element.17.x_ref.refs_2_, f32[384,128]{1,0:T(8,128)S(1)} %get-tuple-element.18.own_even.refs_3_, ...), custom_call_target="tpu_custom_call" | custom-call | flops 40000000 | bytes 2000000 | tf_op jit(solution)/shard_map/interior_early/pallas_call | solution.py:543
  12.6 5.9 %collective-permute-start.3 = (f32[24,128]{1,0:T(8,128)S(1)}, f32[24,128]{1,0:T(8,128)S(1)}, u32[]{:S(2)}, u32[]{:S(2)}) collective-permute-start(f32[24,128]{1,0:T(8,128)S(1)} %get-tuple-element.27), channel_id=1, source_target_pairs={{1,2},{2,1},{3,4},{4,3},{5,6},{6,5},{7,8},{8,7},{9,10},{10,9},{11,... | collective-permute-start | bytes 36872 | tf_op jit(solution)/shard_map/ppermute | solution.py:553
  18.5 2.2 %interior_late.1 = (f32[4,4,16,8,128]{4,3,2,1,0:T(8,128)}, f32[8,32,128]{2,1,0:T(8,128)S(1)}) custom-call(bf16[3,3,256,256]{3,2,1,0:T(8,128)(2,1)S(1)} %copy-done, bf16[3,256,256]{2,1,0:T(8,128)(2,1)S(1)} %copy-done.1, f32[64,32,128]{2,1,0:T(8,128)S(1)} %get-tuple-element.17.x_ref.refs_2_, ...), custom_call_target="tpu_custom_call", output_to_operand_aliasing={{1}: (7, {})} | custom-call | flops 40000000 | bytes 2000000 | tf_op jit(solution)/shard_map/interior_late/pallas_call | solution.py:554
  20.6 0.0 collective-permute-done.2.got_even
  20.6 0.0 collective-permute-done.3.got_odd
  20.6 1.0 %edge_columns.1 = f32[4,4,16,8,128]{4,3,2,1,0:T(8,128)} custom-call(bf16[3,3,256,256]{3,2,1,0:T(8,128)(2,1)S(1)} %copy-done, f32[8,7,8,128]{3,2,1,0:T(8,128)S(1)} %get-tuple-element.20.v_ref, f32[8,32,128]{2,1,0:T(8,128)S(1)} %get-tuple-element.25.edge_in, f32[24,128]{1,0:T(8,128)S(1)} %collective-permute-done.2.got_even, ...), custom_call_target="tpu_custom_call", output_to_operand_aliasing={{}: (5, {})} | custom-call | tf_op jit(solution)/shard_map/edge_columns/pallas_call | solution.py:565
Async XLA Ops:
  1.9 9.5 %copy-start = (bf16[3,3,256,256]{3,2,1,0:T(8,128)(2,1)S(1)}, bf16[3,3,256,256]{3,2,1,0:T(8,128)(2,1)}, u32[]{:S(2)}) copy-start(bf16[3,3,256,256]{3,2,1,0:T(8,128)(2,1)} %constant.4.clone.refs_0_.w_ref) | copy-start | bytes 3538948
  1.9 9.4 %copy-start.1 = (bf16[3,256,256]{2,1,0:T(8,128)(2,1)S(1)}, bf16[3,256,256]{2,1,0:T(8,128)(2,1)}, u32[]{:S(2)}) copy-start(bf16[3,256,256]{2,1,0:T(8,128)(2,1)} %constant.5.clone.refs_1_) | copy-start | bytes 1179652
  1.9 2.6 %collective-permute-start = (f32[384,128]{1,0:T(8,128)S(1)}, f32[384,128]{1,0:T(8,128)S(1)}, u32[]{:S(2)}, u32[]{:S(2)}) collective-permute-start(f32[384,128]{1,0:T(8,128)S(1)} %get-tuple-element.18.own_even.refs_3_), channel_id=1, source_target_pairs={{0,32},{32,0},{64,96},{96,64},{128,160},{160,128},{192,224},{224,1... | collective-permute-start | bytes 589832 | tf_op jit(solution)/shard_map/ppermute | solution.py:488
  2.0 7.1 %collective-permute-start.1 = (f32[384,128]{1,0:T(8,128)S(1)}, f32[384,128]{1,0:T(8,128)S(1)}, u32[]{:S(2)}, u32[]{:S(2)}) collective-permute-start(f32[384,128]{1,0:T(8,128)S(1)} %get-tuple-element.19.own_odd.refs_4_), channel_id=1, source_target_pairs={{32,64},{64,32},{96,128},{128,96},{160,192},{192,160},{0,0},{224,2... | collective-permute-start | bytes 589832 | tf_op jit(solution)/shard_map/ppermute | solution.py:487
  9.4 11.3 %collective-permute-start.2 = (f32[24,128]{1,0:T(8,128)S(1)}, f32[24,128]{1,0:T(8,128)S(1)}, u32[]{:S(2)}, u32[]{:S(2)}) collective-permute-start(f32[24,128]{1,0:T(8,128)S(1)} %get-tuple-element.26), channel_id=1, source_target_pairs={{0,1},{1,0},{2,3},{3,2},{4,5},{5,4},{6,7},{7,6},{8,9},{9,8},{10,11... | collective-permute-start | bytes 36872 | tf_op jit(solution)/shard_map/ppermute | solution.py:542
  12.6 8.0 %collective-permute-start.3 = (f32[24,128]{1,0:T(8,128)S(1)}, f32[24,128]{1,0:T(8,128)S(1)}, u32[]{:S(2)}, u32[]{:S(2)}) collective-permute-start(f32[24,128]{1,0:T(8,128)S(1)} %get-tuple-element.27), channel_id=1, source_target_pairs={{1,2},{2,1},{3,4},{4,3},{5,6},{6,5},{7,8},{8,7},{9,10},{10,9},{11,... | collective-permute-start | bytes 36872 | tf_op jit(solution)/shard_map/ppermute | solution.py:553
